TPU v7x, 256 devices: a whole 4x4x8 slice. The times are simulated.
256 devices in a mesh: row: 32 (over z_lo, y, core), col: 8 (over x, z_hi).
Axes of the slice: x: 4, y: 4, z: 8 (z_hi: 2, z_lo: 4; z = z_hi * 4 + z_lo), core: 2. Of those that a mesh axis runs over, the one named last changes fastest.
Arguments:
- pair_rep: bfloat16 [2048, 2048, 128], P('row', 'col'), may hold values from -6 to 6
- bias_weight: bfloat16 [128, 12], replicated, may hold values from -0.5 to 0.5
- head_weight: float32 [12], replicated, may hold values from -1 to 1
- queries: float32 [192, 2048], P(None, 'row'), may hold values from -48 to 48, as said below
- key_vectors: float32 [192, 2048], P(None, 'col'), may hold values from -48 to 48, as said below
- values: float32 [192, 2048], P(None, 'col'), may hold values from -6 to 6
- query_points: float32 [3, 48, 2048], P(None, None, 'row'), may hold values from -6 to 6
- key_points: float32 [3, 48, 2048], P(None, None, 'col'), may hold values from -6 to 6
- value_points: float32 [3, 96, 2048], P(None, None, 'col'), may hold values from -6 to 6
- rotations: float32 [3, 3, 2048], replicated, may hold values from -1 to 1, as said below
- translations: float32 [3, 2048], replicated, may hold values from -12 to 12
- residue_count: int32 [1], replicated, may hold values from 1024 to 2048
- grad_output: float32 [192, 2048], P(None, 'row'), may hold values from -6 to 6
- grad_points: float32 [3, 96, 2048], P(None, None, 'row'), may hold values from -6 to 6
- grad_pair: bfloat16 [2048, 12, 128], P('row'), may hold values from -2 to 2
Outputs:
- pair_grad: bfloat16 [2048, 2048, 128], P('row', 'col')
- query_grad: float32 [192, 2048], P(None, ('row', 'col'))
- query_point_grad: float32 [3, 48, 2048], P(None, None, ('row', 'col'))
- query_frame_grad: float32 [3, 4, 2048], P(None, None, ('row', 'col'))
- key_grad: float32 [192, 2048], P(None, ('col', 'row'))
- value_grad: float32 [192, 2048], P(None, ('col', 'row'))
- key_point_grad: float32 [3, 48, 2048], P(None, None, ('col', 'row'))
- value_point_grad: float32 [3, 96, 2048], P(None, None, ('col', 'row'))
- key_frame_grad: float32 [3, 4, 2048], P(None, None, ('col', 'row'))
- bias_weight_grad: float32 [128, 12], replicated
- head_weight_grad: float32 [12], replicated
Inputs may be any that keep to these rules, and one draw needn't show every extreme that they name: `queries`: entries of order one, except a few residues whose vectors are much larger. `key_vectors`: entries of order one, except a few residues whose vectors are much larger. `rotations`: each residue's 3 x 3 matrix is a rotation: orthonormal with determinant one.
All inputs are finite; a program needn't handle non-finite values.
Results may differ from a plain program's by a relative error of at most 0.0049.
Values sent between devices are 32-bit elements; how exact they have to be, the bound alone decides.
A program may use at most 128 MiB of HBM per device.

v0:
```python
import functools
import math

import jax
import jax.numpy as jnp
from jax import lax
from jax.experimental import pallas as pl
from jax.experimental.pallas import tpu as pltpu
from jax.sharding import PartitionSpec as P

F32 = jnp.float32
BF16 = jnp.bfloat16
PAD = 16
VMEM_LIMIT = 60 * 1024 * 1024


def dot(a, b, dims):
    return lax.dot_general(a, b, (dims, ((), ())), preferred_element_type=F32)


TN = ((0,), (0,))
NT = ((1,), (1,))
NN = ((1,), (0,))


def split2(x):
    hi = x.astype(BF16)
    return hi, (x - hi.astype(F32)).astype(BF16)


def split3(x):
    hi = x.astype(BF16)
    rest = x - hi.astype(F32)
    mid = rest.astype(BF16)
    return hi, mid, (rest - mid.astype(F32)).astype(BF16)


def forward_kernel(
    heads, block, scale, limit_ref, pair, bias_w, gpair, qcat, kcat, gcat, vcat,
    e_out, d_out, stat_out, lbase, dbase, rows_buf,
):
    step = pl.program_id(0)

    @pl.when(step == 0)
    def _():
        def head(h, carry):
            q0, q1, q2 = split3(qcat[h])
            k0, k1, k2 = split3(kcat[h])
            lbase[h] = dot(
                jnp.concatenate([q0, q0, q1, q0, q2, q1], 0),
                jnp.concatenate([k0, k1, k0, k2, k0, k1], 0),
                TN,
            )
            g0, g1 = split2(gcat[h])
            v0, v1 = split2(vcat[h])
            dbase[h] = dot(
                jnp.concatenate([g0, g0, g1], 0), jnp.concatenate([v0, v1, v0], 0), TN
            )
            return carry

        lax.fori_loop(0, heads, head, 0)

    for r in range(block):
        w = jnp.concatenate([bias_w[...], gpair[r]], 0)
        rows_buf[r] = dot(w, pair[r], NT)
    cols = pair.shape[1]
    rows = pl.ds(pl.multiple_of(step * block, block), block)
    valid = lax.broadcasted_iota(jnp.int32, (block, cols), 1) < limit_ref[0]
    lane = lax.broadcasted_iota(jnp.int32, (block, 128), 1)
    packed = jnp.ones((block, 128), F32)
    for h in range(heads):
        logit = lbase[h, rows, :] + scale * rows_buf[:, h, :]
        logit = jnp.where(valid, logit, F32(-1000000000.0))
        peak = jnp.max(logit, axis=1, keepdims=True)
        e = jnp.exp(logit - peak)
        d = dbase[h, rows, :] + rows_buf[:, PAD + h, :]
        e_out[h] = e
        d_out[h] = d
        packed = jnp.where(lane == h, peak, packed)
        packed = jnp.where(lane == PAD + h, jnp.sum(e, axis=1, keepdims=True), packed)
        packed = jnp.where(lane == 2 * PAD + h, jnp.sum(e * d, axis=1, keepdims=True), packed)
    stat_out[...] = packed


def merged(stats, own):
    peers = stats.shape[0]
    top = stats[0]
    for c in range(1, peers):
        top = jnp.maximum(top, stats[c])
    total = jnp.zeros_like(top)
    upper = jnp.zeros_like(top)
    for c in range(peers):
        f = jnp.exp(stats[c] - top)
        total = total + pltpu.roll(stats[c], 128 - PAD, 1) * f
        upper = upper + pltpu.roll(stats[c], 128 - 2 * PAD, 1) * f
    return jnp.exp(own - top) / total, upper / total


def sums_kernel(
    nq, nv, vwidth, e_in, d_in, stats, own, qcat, kcat, gcat, vcat, key_out, query_out
):
    h = pl.program_id(0)
    factor, delta = merged(stats, own[...])
    mine = lax.broadcasted_iota(jnp.int32, factor.shape, 1) == h
    pick = lambda x: jnp.sum(jnp.where(mine, x, 0.0), axis=1, keepdims=True)
    att = e_in[0] * pick(factor)
    dl = att * (d_in[0] - pick(delta))
    a0, a1 = split2(att)
    d0, d1 = split2(dl)
    q = jnp.concatenate(split2(qcat[0]), 0)
    k = jnp.concatenate(split2(kcat[0]), 0)
    g = jnp.concatenate(split2(gcat[0]), 0)
    v = jnp.concatenate(split2(vcat[0]), 0)
    kk = dot(q, d0, NN) + dot(q, d1, NN)
    key_out[0, :nq, :] = kk[:nq] + kk[nq:]
    vv = dot(g, a0, NN) + dot(g, a1, NN)
    half = g.shape[0] // 2
    key_out[0, nq:, :] = vv[:nv] + vv[half : half + nv]
    qq = dot(k, d0, NT) + dot(k, d1, NT)
    query_out[0, :nq, :] = qq[:nq] + qq[nq:]
    oo = dot(v, a0, NT) + dot(v, a1, NT)
    query_out[0, nq:, :] = oo[vwidth:nv] + oo[half + vwidth : half + nv]


def pair_kernel(
    heads, block, pair, e_in, d_in, stats, own, scaled, gpair, pg_out, w_out, rows_buf
):
    @pl.when(pl.program_id(0) == 0)
    def _():
        rows_buf[...] = jnp.zeros_like(rows_buf)
        w_out[...] = jnp.zeros_like(w_out)

    factor, delta = merged(stats, own[...])
    w_hi, w_lo = split2(scaled[...])
    for h in range(heads):
        att = e_in[h] * factor[:, h : h + 1]
        rows_buf[:, h, :] = att * (d_in[h] - delta[:, h : h + 1])
        rows_buf[:, PAD + h, :] = att
    acc = w_out[...]
    for r in range(block):
        a = rows_buf[r].astype(BF16)
        lhs = jnp.concatenate([a, a[:PAD]], 0)
        rhs = jnp.concatenate([w_hi, gpair[r], w_lo], 0)
        pg_out[r] = dot(lhs, rhs, TN).astype(BF16)
        acc = acc + dot(a[:PAD], pair[r], NN)
    w_out[...] = acc


def push_kernel(axes, sizes, total, x, out, slots, send, recv):
    count = math.prod(sizes)
    place = 0
    for axis, size in zip(axes, sizes):
        place = place * size + lax.axis_index(axis)
    copies = []
    for step in range(1, count):
        peer = lax.rem(place + step, count)
        device = {}
        rest = peer
        for axis, size in reversed(list(zip(axes, sizes))):
            device[axis] = lax.rem(rest, size)
            rest = rest // size
        copy = pltpu.make_async_remote_copy(
            src_ref=x,
            dst_ref=slots.at[place],
            send_sem=send.at[step],
            recv_sem=recv.at[place],
            device_id=device,
            device_id_type=pl.DeviceIdType.MESH,
        )
        copy.start()
        copies.append(copy)
    slots[place] = x[...]
    for step in range(1, count):
        source = lax.rem(place + step, count)
        pltpu.make_async_remote_copy(
            src_ref=x,
            dst_ref=slots.at[source],
            send_sem=send.at[step],
            recv_sem=recv.at[source],
            device_id=device,
            device_id_type=pl.DeviceIdType.MESH,
        ).wait_recv()
    for copy in copies:
        copy.wait_send()
    if total:
        acc = slots[0]
        for c in range(1, count):
            acc = acc + slots[c]
        out[...] = acc
    else:
        out[...] = slots[...]


def pushed(x, axes, total):
    sizes = tuple(lax.axis_size(axis) for axis in axes)
    count = math.prod(sizes)
    return pl.pallas_call(
        functools.partial(push_kernel, axes, sizes, total),
        in_specs=[pl.BlockSpec(memory_space=pltpu.VMEM)],
        out_specs=pl.BlockSpec(memory_space=pltpu.VMEM),
        out_shape=jax.ShapeDtypeStruct(x.shape if total else (count, *x.shape), F32),
        scratch_shapes=[
            pltpu.VMEM((count, *x.shape), F32),
            pltpu.SemaphoreType.DMA((count,)),
            pltpu.SemaphoreType.DMA((count,)),
        ],
        compiler_params=pltpu.CompilerParams(has_side_effects=True),
    )(x)


def turn(rotation, local):
    return jnp.sum(rotation[:, :, None, :] * local[None], axis=1)


def turn_back(rotation, vector):
    return jnp.sum(rotation[:, :, None, :] * vector[:, None], axis=0)


def frame_terms(grad_global, local):
    rotation_part = jnp.sum(grad_global[:, None] * local[None], axis=2)
    return jnp.concatenate([rotation_part, jnp.sum(grad_global, axis=1)[:, None, :]], axis=1)


def by_head(x, heads):
    points = x.shape[1] // heads
    return x.reshape(3, heads, points, -1).transpose(1, 0, 2, 3).reshape(heads, 3 * points, -1)


def by_axis(x):
    heads, rows, m = x.shape
    return x.reshape(heads, 3, rows // 3, m).transpose(1, 0, 2, 3).reshape(3, heads * rows // 3, m)


def pad_rows(x, rows):
    return jnp.pad(x, ((0, 0), (0, rows - x.shape[1]), (0, 0)))


def per_device(
    pair_rep, bias_weight, head_weight, queries, key_vectors, values, query_points, key_points,
    value_points, rotations, translations, residue_count, grad_output, grad_points, grad_pair,
):
    channels, heads = bias_weight.shape
    width = queries.shape[0] // heads
    qpoints = query_points.shape[1] // heads
    vpoints = value_points.shape[1] // heads
    n_rows = queries.shape[1]
    n_cols = key_vectors.shape[1]
    logit_scale = math.sqrt(1.0 / 3.0)
    point_scale = math.sqrt(2.0 / (9.0 * qpoints))
    inner_scale = 1.0 / math.sqrt(width)
    coef = 0.5 * logit_scale * point_scale * jax.nn.softplus(head_weight)
    row_start = lax.axis_index("row") * n_rows
    col_start = lax.axis_index("col") * n_cols
    rot_rows = lax.dynamic_slice_in_dim(rotations, row_start, n_rows, 2)
    shift_rows = lax.dynamic_slice_in_dim(translations, row_start, n_rows, 1)
    rot_cols = lax.dynamic_slice_in_dim(rotations, col_start, n_cols, 2)
    shift_cols = lax.dynamic_slice_in_dim(translations, col_start, n_cols, 1)
    qg = by_head(turn(rot_rows, query_points) + shift_rows[:, None, :], heads)
    kg = by_head(turn(rot_cols, key_points) + shift_cols[:, None, :], heads)
    vg = by_head(turn(rot_cols, value_points) + shift_cols[:, None, :], heads)
    grad_flat = turn(rot_rows, grad_points)
    gg = by_head(grad_flat, heads)
    q = queries.reshape(heads, width, n_rows)
    k = key_vectors.reshape(heads, width, n_cols)
    qsize = width + 3 * qpoints
    nq = -(-(qsize + 2) // 16) * 16
    nv = width + 3 * vpoints
    nvp = -(-nv // 16) * 16
    c3 = coef[:, None, None]
    q_square = jnp.sum(qg * qg, axis=1, keepdims=True)
    k_square = jnp.sum(kg * kg, axis=1, keepdims=True)
    qcat = pad_rows(
        jnp.concatenate(
            [
                logit_scale * inner_scale * q,
                2.0 * c3 * qg,
                jnp.broadcast_to(-c3, (heads, 1, n_rows)),
                -c3 * q_square,
            ],
            axis=1,
        ),
        nq,
    )
    kcat = pad_rows(
        jnp.concatenate([k, kg, k_square, jnp.ones((heads, 1, n_cols), F32)], axis=1), nq
    )
    gcat = pad_rows(
        jnp.concatenate([grad_output.reshape(heads, width, n_rows), gg], axis=1), nvp
    )
    vcat = pad_rows(jnp.concatenate([values.reshape(heads, width, n_cols), vg], axis=1), nvp)
    w_t = jnp.pad(bias_weight.T, ((0, PAD - heads), (0, 0)))
    scaled = logit_scale * w_t.astype(F32)
    gpair = pad_rows(grad_pair, PAD)
    limit = residue_count - col_start

    block = 8
    grid = (n_rows // block,)
    whole = lambda *shape: pl.BlockSpec(shape, lambda i: (0,) * len(shape))
    pair_spec = pl.BlockSpec((block, n_cols, channels), lambda i: (i, 0, 0))
    gpair_spec = pl.BlockSpec((block, PAD, channels), lambda i: (i, 0, 0))
    hij_spec = pl.BlockSpec((heads, block, n_cols), lambda i: (0, i, 0))
    stat_spec = pl.BlockSpec((block, 128), lambda i: (i, 0))
    cat_specs = [
        whole(heads, nq, n_rows),
        whole(heads, nq, n_cols),
        whole(heads, nvp, n_rows),
        whole(heads, nvp, n_cols),
    ]
    params = pltpu.CompilerParams(
        dimension_semantics=("arbitrary",), vmem_limit_bytes=VMEM_LIMIT
    )
    hij = jax.ShapeDtypeStruct((heads, n_rows, n_cols), F32)
    e_all, d_all, own = pl.pallas_call(
        functools.partial(forward_kernel, heads, block, logit_scale),
        grid=grid,
        in_specs=[
            pl.BlockSpec(memory_space=pltpu.SMEM),
            pair_spec,
            whole(PAD, channels),
            gpair_spec,
            *cat_specs,
        ],
        out_specs=[hij_spec, hij_spec, stat_spec],
        out_shape=[hij, hij, jax.ShapeDtypeStruct((n_rows, 128), F32)],
        scratch_shapes=[
            pltpu.VMEM((heads, n_rows, n_cols), F32),
            pltpu.VMEM((heads, n_rows, n_cols), F32),
            pltpu.VMEM((block, 2 * PAD, n_cols), F32),
        ],
        compiler_params=params,
    )(limit, pair_rep, w_t, gpair, qcat, kcat, gcat, vcat)

    stats = pushed(own, ("col",), False)
    peers = stats.shape[0]
    nk = nq + nv
    nr = nq + nv - width
    per_head = lambda *shape: pl.BlockSpec((1, *shape), lambda i: (i, 0, 0))
    key_out, query_out = pl.pallas_call(
        functools.partial(sums_kernel, nq, nv, width),
        grid=(heads,),
        in_specs=[
            per_head(n_rows, n_cols),
            per_head(n_rows, n_cols),
            whole(peers, n_rows, 128),
            whole(n_rows, 128),
            per_head(nq, n_rows),
            per_head(nq, n_cols),
            per_head(nvp, n_rows),
            per_head(nvp, n_cols),
        ],
        out_specs=[per_head(nk, n_cols), per_head(nr, n_rows)],
        out_shape=[
            jax.ShapeDtypeStruct((heads, nk, n_cols), F32),
            jax.ShapeDtypeStruct((heads, nr, n_rows), F32),
        ],
        compiler_params=params,
    )(e_all, d_all, stats, own, qcat, kcat, gcat, vcat)
    key_sum = lax.psum_scatter(
        key_out.reshape(heads * nk, n_cols), "row", scatter_dimension=1, tiled=True
    ).reshape(heads, nk, -1)
    query_sum = lax.psum_scatter(
        query_out.reshape(heads * nr, n_rows), "col", scatter_dimension=1, tiled=True
    ).reshape(heads, nr, -1)
    pair_grad, w_out = pl.pallas_call(
        functools.partial(pair_kernel, heads, block),
        grid=grid,
        in_specs=[
            pair_spec,
            hij_spec,
            hij_spec,
            pl.BlockSpec((peers, block, 128), lambda i: (0, i, 0)),
            stat_spec,
            whole(PAD, channels),
            gpair_spec,
        ],
        out_specs=[pair_spec, whole(PAD, channels)],
        out_shape=[
            jax.ShapeDtypeStruct(pair_rep.shape, BF16),
            jax.ShapeDtypeStruct((PAD, channels), F32),
        ],
        scratch_shapes=[pltpu.VMEM((block, 2 * PAD, n_cols), F32)],
        compiler_params=params,
        cost_estimate=pl.CostEstimate(
            flops=8 * n_rows * n_cols * channels * PAD,
            bytes_accessed=4 * n_rows * n_cols * channels + 8 * heads * n_rows * n_cols,
            transcendentals=0,
        ),
    )(pair_rep, e_all, d_all, stats, own, scaled, gpair)

    distance_part = jnp.sum(
        q_square[:, 0] * query_out[:, qsize + 1] + query_out[:, qsize], axis=1
    ) - 2.0 * jnp.sum(qg * query_out[:, width:qsize], axis=(1, 2))
    small = jnp.concatenate(
        [logit_scale * w_out, jnp.pad(distance_part, (0, 8 * channels - heads)).reshape(8, channels)]
    )
    small = pushed(small, ("row", "col"), True)
    weight_total = small[:heads].T
    head_weight_grad = (
        small[PAD, :heads] * (-0.5 * logit_scale * point_scale) * jax.nn.sigmoid(head_weight)
    )

    share = query_sum.shape[2]
    start = lax.axis_index("col") * share
    own_rows = lambda x: lax.dynamic_slice_in_dim(x, start, share, x.ndim - 1)
    rot_own = own_rows(rot_rows)
    shift_own = own_rows(shift_rows)
    query_grad = (logit_scale * inner_scale * query_sum[:, :width]).reshape(heads * width, share)
    dqg = by_axis(
        -2.0 * c3 * (own_rows(qg) * query_sum[:, qsize + 1][:, None] - query_sum[:, width:qsize])
    )
    point_out = by_axis(query_sum[:, nq:])
    query_point_grad = turn_back(rot_own, dqg)
    cotan_own = own_rows(grad_points)
    out_part = jnp.sum((point_out - shift_own[:, None, :])[:, None] * cotan_own[None], axis=2)
    out_part = jnp.concatenate(
        [out_part, -jnp.sum(own_rows(grad_flat), axis=1)[:, None, :]], axis=1
    )
    query_frame_grad = frame_terms(dqg, own_rows(query_points)) + out_part

    kshare = key_sum.shape[2]
    kstart = lax.axis_index("row") * kshare
    own_cols = lambda x: lax.dynamic_slice_in_dim(x, kstart, kshare, x.ndim - 1)
    rot_keys = own_cols(rot_cols)
    key_grad = key_sum[:, :width].reshape(heads * width, kshare)
    value_grad = key_sum[:, nq : nq + width].reshape(heads * width, kshare)
    dkg = by_axis(
        key_sum[:, width:qsize] + 2.0 * own_cols(kg) * key_sum[:, qsize][:, None]
    )
    dvg = by_axis(key_sum[:, nq + width :])
    key_point_grad = turn_back(rot_keys, dkg)
    value_point_grad = turn_back(rot_keys, dvg)
    key_frame_grad = frame_terms(dkg, own_cols(key_points)) + frame_terms(
        dvg, own_cols(value_points)
    )
    return (
        pair_grad, query_grad, query_point_grad, query_frame_grad, key_grad, value_grad,
        key_point_grad, value_point_grad, key_frame_grad, weight_total, head_weight_grad,
    )


def solution(mesh):
    return jax.shard_map(
        per_device,
        mesh=mesh,
        in_specs=(
            P("row", "col", None),
            P(),
            P(),
            P(None, "row"),
            P(None, "col"),
            P(None, "col"),
            P(None, None, "row"),
            P(None, None, "col"),
            P(None, None, "col"),
            P(),
            P(),
            P(),
            P(None, "row"),
            P(None, None, "row"),
            P("row", None, None),
        ),
        out_specs=(
            P("row", "col", None),
            P(None, ("row", "col")),
            P(None, None, ("row", "col")),
            P(None, None, ("row", "col")),
            P(None, ("col", "row")),
            P(None, ("col", "row")),
            P(None, None, ("col", "row")),
            P(None, None, ("col", "row")),
            P(None, None, ("col", "row")),
            P(),
            P(),
        ),
        check_vma=False,
    )
```

profile of v0, /device:TPU:1, one launch (start us, length us, event | category | flops | bytes accessed | tf_op | source)
XLA Modules:
  0.0 374.9 jit_solution(10862487212332247991)
XLA Ops:
  8.1 0.7 copy-done
  8.8 0.8 constant_dynamic-slice_fusion.10
  9.6 0.7 constant_dynamic-slice_fusion.8
  11.0 0.7 broadcast_multiply_fusion.3
  11.7 0.9 broadcast_multiply_fusion.1
  12.5 0.1 copy.137
  12.6 0.9 multiply_reduce_fusion.3
  13.6 1.0 multiply_reduce_fusion.2
  14.7 0.1 copy.141
  14.8 0.9 copy.140
  15.8 1.0 multiply_reduce_fusion.1
  16.9 1.1 copy.136
  18.0 1.3 pad.28.bias_w
  19.3 0.7 pad.29.gpair
  20.4 0.8 select_maximum_fusion.1.gcat
  21.1 0.9 select_maximum_fusion.vcat
  22.0 0.1 maximum_maximum_fusion
  22.1 0.8 pad.31.kcat
  23.0 0.7 select_maximum_fusion.2.qcat
  23.7 10.4 %shard_map.230 = (f32[12,64,256]{2,1,0:T(8,128)}, f32[12,64,256]{2,1,0:T(8,128)}, f32[64,128]{1,0:T(8,128)}) custom-call(s32[1]{0:T(128)S(6)} %sub.25.limit_ref, bf16[64,256,128]{2,1,0:T(8,128)(2,1)} %pair.3, bf16[16,128]{1,0:T(8,128)(2,1)} %pad.28.bias_w, bf16[64,16,128]{2,1,0:T(8,128)(2,1)} %pad.29.gpair, f32[12,32,64]{2,1,0:T(8,128)} %select_maximum_fusion.2.qcat, ...), custom_call_target="tpu_custom_call" | custom-call | tf_op jit(solution)/shard_map/pallas_call | solution.py:313
  34.1 28.1 %shard_map.231.stats = f32[8,64,128]{2,1,0:T(8,128)} custom-call(f32[64,128]{1,0:T(8,128)} %get-tuple-element.20.x.own), custom_call_target="tpu_custom_call" | custom-call | tf_op jit(solution)/shard_map/pallas_call | solution.py:197
  62.2 10.2 %shard_map.233 = (f32[12,72,256]{2,1,0:T(8,128)}, f32[12,56,64]{2,1,0:T(8,128)}) custom-call(f32[12,64,256]{2,1,0:T(8,128)} %get-tuple-element.18.e_in, f32[12,64,256]{2,1,0:T(8,128)} %get-tuple-element.19.d_in, f32[8,64,128]{2,1,0:T(8,128)} %shard_map.231.stats, f32[64,128]{1,0:T(8,128)} %get-tuple-element.20.x.own, ...), custom_call_target="tpu_custom_call" | custom-call | tf_op jit(solution)/shard_map/pallas_call | solution.py:338
  72.4 1.8 copy.169
  74.3 0.5 all-reduce.10.cloned.1.call-update
  74.9 0.6 convert_multiply_fusion.scaled
  75.6 0.8 dynamic-slice_reduce_fusion
  76.4 0.1 constant_dynamic-slice_fusion.1
  76.5 0.1 constant_dynamic-slice_fusion
  76.6 1.1 multiply_reduce_fusion.5
  77.7 1.1 copy.164
  78.7 0.1 fusion.3
  78.9 9.3 %shard_map.232 = (bf16[64,256,128]{2,1,0:T(8,128)(2,1)}, f32[16,128]{1,0:T(8,128)}) custom-call(bf16[64,256,128]{2,1,0:T(8,128)(2,1)} %pair.3, f32[12,64,256]{2,1,0:T(8,128)} %get-tuple-element.18.e_in, f32[12,64,256]{2,1,0:T(8,128)} %get-tuple-element.19.d_in, f32[8,64,128]{2,1,0:T(8,128)} %shard_map.231.stats, f32[64,128]{1,0:T(8,128)} %get-tuple-element.20.x.own, ...), custom_call_target="tpu_custom_call" | custom-call | flops 268435456 | bytes 9961472 | tf_op jit(solution)/shard_map/pallas_call | solution.py:364
  88.1 0.7 broadcast_multiply_fusion.2
  88.8 0.6 pad_maximum_fusion.x
  89.4 94.2 %shard_map.234 = f32[24,128]{1,0:T(8,128)} custom-call(f32[24,128]{1,0:T(8,128)} %pad_maximum_fusion.x), custom_call_target="tpu_custom_call" | custom-call | tf_op jit(solution)/shard_map/pallas_call | solution.py:197
  183.7 1.2 divide_multiply_fusion
  184.9 1.3 slice_bitcast_fusion.4
  186.2 0.9 constant_dynamic-slice_fusion.2
  187.2 0.1 copy.162
  187.3 0.6 dynamic-slice
  188.6 0.9 copy.170
  189.6 0.1 fusion.1
  189.7 0.1 copy.146
  189.8 0.1 reduce_sum.191
  189.9 0.1 copy.147
  190.2 0.7 copy.166
  190.8 0.1 copy.151
  191.0 0.1 reshape.178
  191.2 0.1 multiply_reduce_fusion.11
  191.3 169.9 %all-reduce.10.cloned.1.call-done = f32[864,256]{1,0:T(8,128)} async-done(((f32[864,256]{1,0:T(8,128)}), f32[864,256]{1,0:T(8,128)}) %all-reduce.10.cloned.1.call-update) | async-done | bytes 884752
  361.2 1.2 constant_dynamic-slice_fusion.11
  362.4 0.1 slice_add_fusion
  362.5 0.1 copy.156
  362.6 0.1 reduce_sum.197
  362.7 0.1 copy.157
  363.0 0.7 copy.168
  363.7 0.7 copy.167
  364.3 0.1 copy.159
  364.5 0.1 bitcast_reduce_fusion
  364.6 0.1 mul.329
  364.8 0.7 multiply_reduce_fusion.7
  365.5 0.7 multiply_reduce_fusion.8
  366.2 0.6 maximum_add_fusion.1
  366.8 0.6 maximum_add_fusion
  (61 shorter events, 1.6 us)
Async XLA Ops:
  8.0 0.8 copy-start
  8.0 12.0 %copy-start.1 = (f32[3,96,256]{2,1,0:T(8,128)S(1)}, f32[3,96,256]{2,1,0:T(8,128)}, u32[]{:S(2)}) copy-start(f32[3,96,256]{2,1,0:T(8,128)} %param.23) | copy-start | bytes 884740
  8.0 13.1 %copy-start.5 = (f32[192,256]{1,0:T(8,128)S(1)}, f32[192,256]{1,0:T(8,128)}, u32[]{:S(2)}) copy-start(f32[192,256]{1,0:T(8,128)} %param.20) | copy-start | bytes 589828
  8.0 14.0 %copy-start.4 = (f32[192,256]{1,0:T(8,128)S(1)}, f32[192,256]{1,0:T(8,128)}, u32[]{:S(2)}) copy-start(f32[192,256]{1,0:T(8,128)} %param.19) | copy-start | bytes 589828
  8.1 180.6 %reduce-scatter.5.cloned.1.call-start = ((), (), s32[]{:S(2)}) async-start(), calls=%async_computation.1 | async-start | bytes 221184
  23.7 51.2 %copy-start.6 = (bf16[128,12]{0,1:T(8,128)(2,1)S(1)}, bf16[128,12]{0,1:T(8,128)(2,1)}, u32[]{:S(2)}) copy-start(bf16[128,12]{0,1:T(8,128)(2,1)} %param.16) | copy-start | bytes 9220
  23.7 51.8 %copy-start.3 = (f32[3,48,64]{2,1,0:T(8,128)S(1)}, f32[3,48,64]{2,1,0:T(8,128)}, u32[]{:S(2)}) copy-start(f32[3,48,64]{2,1,0:T(8,128)} %param.21) | copy-start | bytes 110596
  34.1 42.3 %copy-start.2 = (f32[3,48,256]{2,1,0:T(8,128)S(1)}, f32[3,48,256]{2,1,0:T(8,128)}, u32[]{:S(2)}) copy-start(f32[3,48,256]{2,1,0:T(8,128)} %param.22) | copy-start | bytes 442372
  74.3 286.9 %all-reduce.10.cloned.1.call-start = ((), (), s32[]{:S(2)}) async-start(), calls=%async_computation.2 | async-start | bytes 1769472
  74.8 108.8 %copy-start.7 = (f32[12]{0:T(128)S(1)}, f32[12]{0:T(128)}, u32[]{:S(2)}) copy-start(f32[12]{0:T(128)} %param.17) | copy-start | bytes 148
  75.6 111.8 %copy-start.8 = (u32[256]{0:T(256)S(1)}, u32[256]{0:T(256)}, u32[]{:S(2)}) copy-start(u32[256]{0:T(256)} %constant.102) | copy-start | bytes 3076
Sparse Core Ops, SparseCore 0:
  74.4 84.6 reduce-scatter.4
Sparse Core Ops, SparseCore 1:
  77.4 283.7 all-reduce.9
where the time goes:
time: 377 us; the launch traced here: 375 us
  waiting for transfers between devices  170 us (45%)
  Pallas kernels  152 us (40%)
  local copies, waits for them, and re-layouts  19.2 us (5%)
  between operations  17.2 us (5%)
  other arithmetic  15.8 us (4%)
    unnamed x4, waiting for transfers between devices  170 us
    pallas_call x2, Pallas kernels, pushed(): pl.pallas_call(functools.partial(push_kernel, axes, sizes, total), in_spe...  122 us
    pallas_call x1, Pallas kernels, per_device(): pl.pallas_call(functools.partial(forward_kernel, heads, block, logit_scal...  10.4 us
    pallas_call x1, Pallas kernels, per_device(): pl.pallas_call(functools.partial(sums_kernel, nq, nv, width), grid=(heads...  10.2 us
    pallas_call x1, Pallas kernels, per_device(): pl.pallas_call(functools.partial(pair_kernel, heads, block), grid=grid, i...  9.27 us
    unnamed x27, local copies, waits for them, and re-layouts  9.21 us
  transfers between devices with their start and end apart: 2, of which 1 were waited for; matrix products, arithmetic and copies ran while one was open for 3% of the time, Pallas kernels for 28%

commit v1 on v0

v1 whole, which is shorter than its diff:
```python
import functools
import math

import jax
import jax.numpy as jnp
from jax import lax
from jax.experimental import pallas as pl
from jax.experimental.pallas import tpu as pltpu
from jax.sharding import PartitionSpec as P

F32 = jnp.float32
BF16 = jnp.bfloat16
PAD = 16
VMEM_LIMIT = 48 * 1024 * 1024
ZL, YN, CORES = 4, 4, 2
XN, ZH = 4, 2
STRIDE = 40
MESH = pl.DeviceIdType.MESH


def dot(a, b, dims):
    return lax.dot_general(a, b, (dims, ((), ())), preferred_element_type=F32)


TN = ((0,), (0,))
NT = ((1,), (1,))
NN = ((1,), (0,))


def split2(x):
    hi = x.astype(BF16)
    return hi, (x - hi.astype(F32)).astype(BF16)


def split3(x):
    hi = x.astype(BF16)
    rest = x - hi.astype(F32)
    mid = rest.astype(BF16)
    return hi, mid, (rest - mid.astype(F32)).astype(BF16)


def lane_of(shape):
    return lax.broadcasted_iota(jnp.int32, shape, 1)


def merge_stats(parts):
    top = functools.reduce(jnp.maximum, parts)
    lane = lax.rem(lane_of(top.shape), 64)
    out = None
    for part in parts:
        f = jnp.exp(part - top)
        spread = jnp.where(lane < 2 * PAD, pltpu.roll(f, PAD, 1), pltpu.roll(f, 2 * PAD, 1))
        term = part * spread
        out = term if out is None else out + term
    return jnp.where(lane < PAD, top, out)


def push(src, dst, send, recv, row, col):
    copy = pltpu.make_async_remote_copy(
        src_ref=src, dst_ref=dst, send_sem=send, recv_sem=recv,
        device_id={"row": row, "col": col}, device_id_type=MESH,
    )
    copy.start()
    return copy


def mega_kernel(
    heads, n_rows, n_cols, scale,
    rc, pair_hbm, w_t, scaled, gpair, qcat, kcat, gcat, vcat, wq,
    pg_out, kf_out, qf_out, wr_out,
    pair, lbase, dbase, fb0, fb1, rd0, rd1, a_hi, a_lo, d_hi, d_lo,
    qb, gb, stat, stat_z, stat_m, stat_x,
    ks, ks_rx, sy, sy_rx, sz, sz_rx, qs, qs_rx, qz, qz_rx,
    ar_c, ar_y, ar_x, ar_z, ar_s,
    pair_sem, s_send, s_recv, k_send, k_recv, y_send, y_recv, z_send, z_recv,
    q_send, q_recv, a_send, a_recv,
):
    rw = lax.axis_index("row")
    cl = lax.axis_index("col")
    core = lax.rem(rw, CORES)
    yy = lax.rem(rw // CORES, YN)
    zl = rw // (CORES * YN)
    zh = lax.rem(cl, ZH)
    xx = cl // ZH
    row_of = lambda z, y, c: (z * YN + y) * CORES + c
    sibling = (row_of(zl, yy, 1 - core), cl)
    y_peer = lambda k: (row_of(zl, lax.rem(yy + k, YN), core), cl)
    z_peer = lambda k: (row_of(lax.rem(zl + k, ZL), yy, core), cl)
    x_peer = lambda k: (rw, lax.rem(xx + k, XN) * ZH + zh)
    h_peer = (rw, xx * ZH + 1 - zh)
    z8 = zh * ZL + zl

    def ring_peer(k):
        idx = lax.rem(z8 + k, ZL * ZH)
        return (row_of(lax.rem(idx, ZL), yy, core), xx * ZH + idx // ZL)

    everyone = [sibling]
    everyone += [y_peer(k) for k in range(1, YN)]
    everyone += [x_peer(k) for k in range(1, XN)]
    everyone += [ring_peer(k) for k in range(1, ZL * ZH)]
    barrier = pltpu.get_barrier_semaphore()
    for peer in everyone:
        pl.semaphore_signal(
            barrier, inc=1, device_id={"row": peer[0], "col": peer[1]}, device_id_type=MESH
        )

    parts = 4
    rows_per = n_rows // parts
    loads = []
    for p in range(parts):
        piece = pl.ds(p * rows_per, rows_per)
        load = pltpu.make_async_copy(pair_hbm.at[piece], pair.at[piece], pair_sem.at[p])
        load.start()
        loads.append(load)

    for h in range(heads):
        q0, q1, q2 = split3(qcat[h][:, :n_rows])
        k0, k1, k2 = split3(kcat[h])
        lbase[h] = dot(
            jnp.concatenate([q0, q0, q1, q0, q2, q1], 0),
            jnp.concatenate([k0, k1, k0, k2, k0, k1], 0),
            TN,
        )
        g0, g1 = split2(gcat[h][:, :n_rows])
        v0, v1 = split2(vcat[h])
        dbase[h] = dot(
            jnp.concatenate([g0, g0, g1], 0), jnp.concatenate([v0, v1, v0], 0), TN
        )

    for p in range(parts):
        loads[p].wait()

        for i in range(rows_per):
            r = p * rows_per + i
            w = jnp.concatenate([w_t[...], gpair[r]], 0)
            res = dot(w, pair[r], NT)
            fb0[r * STRIDE : r * STRIDE + 2 * PAD, :] = res[:, :128]
            fb1[r * STRIDE : r * STRIDE + 2 * PAD, :] = res[:, 128:]

    limit = rc[0] - cl * n_cols
    valid = lane_of((n_rows, n_cols)) < limit
    lane = lane_of((n_rows, 128))
    packed = jnp.ones((n_rows, 128), F32)
    picked = lambda ref0, ref1, h: jnp.concatenate(
        [ref0[pl.ds(h, n_rows, stride=STRIDE), :], ref1[pl.ds(h, n_rows, stride=STRIDE), :]], 1
    )
    for h in range(heads):
        logit = lbase[h] + scale * picked(fb0, fb1, h)
        logit = jnp.where(valid, logit, F32(-1000000000.0))
        peak = jnp.max(logit, axis=1, keepdims=True)
        e = jnp.exp(logit - peak)
        d = dbase[h] + picked(fb0, fb1, PAD + h)
        lbase[h] = e
        dbase[h] = d
        packed = jnp.where(lane == h, peak, packed)
        packed = jnp.where(lane == PAD + h, jnp.sum(e, axis=1, keepdims=True), packed)
        packed = jnp.where(lane == 2 * PAD + h, jnp.sum(e * d, axis=1, keepdims=True), packed)
    half = n_rows // 2
    own = jnp.where(lane[:half] < 64, packed[:half], pltpu.roll(packed[half:], 64, 1))
    stat[...] = own

    pl.semaphore_wait(barrier, len(everyone))
    sends = []
    sends.append(push(stat, stat_z, s_send.at[0], s_recv.at[0], *h_peer))

    rd0[...] = jnp.zeros_like(rd0)
    rd1[...] = jnp.zeros_like(rd1)
    qb[...] = jnp.zeros_like(qb)
    gb[...] = jnp.zeros_like(gb)
    for h in range(heads):
        g, k = h // 4, h % 4
        x = qcat[h]
        if k % 2:
            x = pltpu.roll(x, 64, 1)
        c0 = 128 * (k // 2)
        hi, lo = split2(x)
        qb[g, 32 * k : 32 * k + 32, c0 : c0 + 128] = hi
        qb[g, 128 + 32 * k : 160 + 32 * k, c0 : c0 + 128] = lo
        g, k = h // 3, h % 3
        x = gcat[h]
        if k % 2:
            x = pltpu.roll(x, 64, 1)
        c0 = 128 * (k // 2)
        hi, lo = split2(x)
        gb[g, 48 * k : 48 * k + 48, c0 : c0 + 128] = hi
        gb[g, 144 + 48 * k : 192 + 48 * k, c0 : c0 + 128] = lo

    def landed(dst, send, recv, peer):
        pltpu.make_async_remote_copy(
            src_ref=dst, dst_ref=dst, send_sem=send, recv_sem=recv,
            device_id={"row": peer[0], "col": peer[1]}, device_id_type=MESH,
        ).wait_recv()

    landed(stat_z, s_send.at[0], s_recv.at[0], h_peer)
    pairwise = merge_stats([stat[...], stat_z[...]])
    stat_m[...] = pairwise
    for k in range(1, XN):
        sends.append(
            push(stat_m, stat_x.at[k - 1], s_send.at[k], s_recv.at[k], *x_peer(k))
        )
    for k in range(1, XN):
        landed(stat_x.at[k - 1], s_send.at[k], s_recv.at[k], x_peer(k))
    total = merge_stats([stat_m[...]] + [stat_x[k] for k in range(XN - 1)])
    mass = pltpu.roll(total, 128 - PAD, 1)
    factor = jnp.exp(stat[...] - total) / mass
    delta = pltpu.roll(total, 128 - 2 * PAD, 1) / mass
    factor = jnp.concatenate([factor, pltpu.roll(factor, 64, 1)], 0)
    delta = jnp.concatenate([delta, pltpu.roll(delta, 64, 1)], 0)

    def make_head(h):
        att = lbase[h] * factor[:, h : h + 1]
        dl = att * (dbase[h] - delta[:, h : h + 1])
        rows = pl.ds(h * n_rows, n_rows)
        a_hi[rows], a_lo[rows] = split2(att)
        d_hi[rows], d_lo[rows] = split2(dl)
        rd0[pl.ds(h, n_rows, stride=STRIDE), :] = dl[:, :128]
        rd1[pl.ds(h, n_rows, stride=STRIDE), :] = dl[:, 128:]
        rd0[pl.ds(PAD + h, n_rows, stride=STRIDE), :] = att[:, :128]
        rd1[pl.ds(PAD + h, n_rows, stride=STRIDE), :] = att[:, 128:]

    def key_group(g, left, hi, lo, first, count, width):
        depth = count * n_rows
        rows = pl.ds(first * n_rows, depth)
        lanes = count * width
        left = left[:, :depth]
        res = dot(left, hi[rows], NN)
        res = res[:lanes] + res[lanes:] + dot(left[:lanes], lo[rows], NN)
        if lanes > 128:
            res = jnp.concatenate([res[width * k : width * k + 40] for k in range(count)], 0)
            res = jnp.concatenate([res, jnp.zeros((8, n_cols), F32)], 0)
        flat = res.T.reshape(ZL * YN, CORES, 8, 128)
        for c in range(CORES):
            ks[g, c] = flat[:, c]
        sends.append(
            push(ks.at[g, 1 - core], ks_rx.at[g], k_send.at[g], k_recv.at[g], *sibling)
        )

    def y_stage(g):
        landed(ks_rx.at[g], k_send.at[g], k_recv.at[g], sibling)
        both = (ks[g, core] + ks_rx[g]).reshape(ZL, YN, 8, 128)
        for y in range(YN):
            sy[y, g] = both[:, y]
        for k in range(1, YN):
            sends.append(
                push(
                    sy.at[lax.rem(yy + k, YN), g], sy_rx.at[k - 1, g],
                    y_send.at[k - 1, g], y_recv.at[k - 1, g], *y_peer(k)
                )
            )

    for h in range(4):
        make_head(h)
    key_group(0, qb[0], d_hi, d_lo, 0, 4, 32)
    key_group(3, gb[0], a_hi, a_lo, 0, 3, 48)
    for h in range(4, 8):
        make_head(h)
    key_group(1, qb[1], d_hi, d_lo, 4, 4, 32)
    key_group(4, gb[1], a_hi, a_lo, 3, 3, 48)
    y_stage(0)
    y_stage(3)
    for h in range(8, 12):
        make_head(h)
    key_group(2, qb[2], d_hi, d_lo, 8, 4, 32)
    key_group(5, gb[2], a_hi, a_lo, 6, 3, 48)
    key_group(6, gb[3], a_hi, a_lo, 9, 3, 48)
    y_stage(1)
    y_stage(4)

    def query_group(source, first, skip):
        hi_cat, lo_cat, left_hi, left_lo = [], [], [], []
        for k in range(4):
            h = first + k
            block = source[h]
            if skip:
                block = jnp.concatenate([block[PAD:40], jnp.zeros((8, n_cols), F32)], 0)
            hi, lo = split2(block)
            zero = lambda n: [jnp.zeros((n, n_cols), BF16)] if n else []
            hi_cat.append(jnp.concatenate(zero(32 * k) + [hi] + zero(96 - 32 * k), 0))
            lo_cat.append(jnp.concatenate(zero(32 * k) + [lo] + zero(96 - 32 * k), 0))
            rows = pl.ds(h * n_rows, n_rows)
            left_hi.append((a_hi if skip else d_hi)[rows])
            left_lo.append((a_lo if skip else d_lo)[rows])
        hi_cat = jnp.concatenate(hi_cat, 1)
        lo_cat = jnp.concatenate(lo_cat, 1)
        left_hi = jnp.concatenate(left_hi, 1)
        left_lo = jnp.concatenate(left_lo, 1)
        res = dot(jnp.concatenate([left_hi, left_lo], 0), hi_cat, NT)
        return res[:n_rows] + res[n_rows:] + dot(left_hi, lo_cat, NT)

    distance = []
    for g in range(6):
        res = query_group(kcat if g < 3 else vcat, 4 * (g % 3), g >= 3)
        if g < 3:
            distance.append(jnp.sum(res * wq[g], axis=0, keepdims=True))
        flat = res.reshape(XN, ZH, 8, 128)
        for x in range(XN):
            for z in range(ZH):
                qs[x, z, g] = flat[x, z]
    for k in range(1, XN):
        sends.append(
            push(
                qs.at[lax.rem(xx + k, XN)], qs_rx.at[k - 1],
                q_send.at[k - 1], q_recv.at[k - 1], *x_peer(k)
            )
        )
    y_stage(2)
    y_stage(5)
    y_stage(6)

    row_block = lambda r: jnp.concatenate(
        [rd0[r * STRIDE : r * STRIDE + 2 * PAD, :], rd1[r * STRIDE : r * STRIDE + 2 * PAD, :]], 1
    ).astype(BF16)
    acc = jnp.zeros((PAD, 128), F32)
    for r in range(n_rows):
        acc = acc + dot(row_block(r)[:PAD], pair[r], NN)
    acc = scale * acc
    sub = lax.broadcasted_iota(jnp.int32, (PAD, 128), 0)
    for g in range(3):
        acc = jnp.where(sub == heads + g, distance[g], acc)
    ar_s[0] = acc
    sends.append(push(ar_s.at[0], ar_c, a_send.at[0], a_recv.at[0], *sibling))

    w_hi, w_lo = split2(scaled[...])

    def pair_rows(first, count):
        for r in range(first, first + count):
            a = row_block(r)
            lhs = jnp.concatenate([a, a[:PAD]], 0)
            rhs = jnp.concatenate([w_hi, gpair[r], w_lo], 0)
            pg_out[r] = dot(lhs, rhs, TN).astype(BF16)

    quarter = n_rows // 4
    pair_rows(0, quarter)

    landed(ar_c, a_send.at[0], a_recv.at[0], sibling)
    ar_s[1] = ar_s[0] + ar_c[...]
    ar_y[yy] = ar_s[1]
    for k in range(1, YN):
        sends.append(push(ar_s.at[1], ar_y.at[yy], a_send.at[k], a_recv.at[k], *y_peer(k)))

    pair_rows(quarter, quarter)

    for k in range(1, XN):
        landed(qs_rx.at[k - 1], q_send.at[k - 1], q_recv.at[k - 1], x_peer(k))
    qz[...] = qs[xx] + qs_rx[0] + qs_rx[1] + qs_rx[2]
    sends.append(push(qz.at[1 - zh], qz_rx, q_send.at[3], q_recv.at[3], *h_peer))

    for k in range(1, YN):
        landed(ar_y.at[lax.rem(yy + YN - k, YN)], a_send.at[k], a_recv.at[k], y_peer(k))
    ar_s[2] = ar_y[0] + ar_y[1] + ar_y[2] + ar_y[3]
    ar_x[xx] = ar_s[2]
    for k in range(1, XN):
        sends.append(
            push(ar_s.at[2], ar_x.at[xx], a_send.at[3 + k], a_recv.at[3 + k], *x_peer(k))
        )

    for g in (0, 3, 1, 4, 2, 5, 6):
        for k in range(1, YN):
            landed(sy_rx.at[k - 1, g], y_send.at[k - 1, g], y_recv.at[k - 1, g], y_peer(k))
        mine = sy[yy, g] + sy_rx[0, g] + sy_rx[1, g] + sy_rx[2, g]
        for z in range(ZL):
            sz[z, g] = mine[z]
    for k in range(1, ZL):
        sends.append(
            push(
                sz.at[lax.rem(zl + k, ZL)], sz_rx.at[k - 1],
                z_send.at[k - 1], z_recv.at[k - 1], *z_peer(k)
            )
        )
    pair_rows(2 * quarter, quarter)

    for k in range(1, XN):
        landed(ar_x.at[lax.rem(xx + XN - k, XN)], a_send.at[3 + k], a_recv.at[3 + k], x_peer(k))
    ar_s[3] = ar_x[0] + ar_x[1] + ar_x[2] + ar_x[3]
    ar_z[z8] = ar_s[3]
    for k in range(1, ZL * ZH):
        sends.append(
            push(ar_s.at[3], ar_z.at[z8], a_send.at[6 + k], a_recv.at[6 + k], *ring_peer(k))
        )

    pair_rows(3 * quarter, quarter)

    for k in range(1, ZL):
        landed(sz_rx.at[k - 1], z_send.at[k - 1], z_recv.at[k - 1], z_peer(k))
    kf_out[...] = sz[zl] + sz_rx[0] + sz_rx[1] + sz_rx[2]
    landed(qz_rx, q_send.at[3], q_recv.at[3], h_peer)
    qf_out[...] = qz[zh] + qz_rx[...]
    for k in range(1, ZL * ZH):
        landed(
            ar_z.at[lax.rem(z8 + ZL * ZH - k, ZL * ZH)], a_send.at[6 + k], a_recv.at[6 + k],
            ring_peer(k),
        )
    grand = ar_z[0]
    for k in range(1, ZL * ZH):
        grand = grand + ar_z[k]
    wr_out[...] = grand
    for copy in sends:
        copy.wait_send()


def turn(rotation, local):
    return jnp.sum(rotation[:, :, None, :] * local[None], axis=1)


def turn_back(rotation, vector):
    return jnp.sum(rotation[:, :, None, :] * vector[:, None], axis=0)


def frame_terms(grad_global, local):
    rotation_part = jnp.sum(grad_global[:, None] * local[None], axis=2)
    return jnp.concatenate([rotation_part, jnp.sum(grad_global, axis=1)[:, None, :]], axis=1)


def by_head(x, heads):
    points = x.shape[1] // heads
    return x.reshape(3, heads, points, -1).transpose(1, 0, 2, 3).reshape(heads, 3 * points, -1)


def by_axis(x):
    heads, rows, m = x.shape
    return x.reshape(heads, 3, rows // 3, m).transpose(1, 0, 2, 3).reshape(3, heads * rows // 3, m)


def pad_to(x, rows, lanes):
    return jnp.pad(x, ((0, 0), (0, rows - x.shape[1]), (0, lanes - x.shape[2])))


def per_device(
    pair_rep, bias_weight, head_weight, queries, key_vectors, values, query_points, key_points,
    value_points, rotations, translations, residue_count, grad_output, grad_points, grad_pair,
):
    channels, heads = bias_weight.shape
    width = queries.shape[0] // heads
    qpoints = query_points.shape[1] // heads
    vpoints = value_points.shape[1] // heads
    n_rows = queries.shape[1]
    n_cols = key_vectors.shape[1]
    logit_scale = math.sqrt(1.0 / 3.0)
    point_scale = math.sqrt(2.0 / (9.0 * qpoints))
    inner_scale = 1.0 / math.sqrt(width)
    coef = 0.5 * logit_scale * point_scale * jax.nn.softplus(head_weight)
    row_start = lax.axis_index("row") * n_rows
    col_start = lax.axis_index("col") * n_cols
    rot_rows = lax.dynamic_slice_in_dim(rotations, row_start, n_rows, 2)
    shift_rows = lax.dynamic_slice_in_dim(translations, row_start, n_rows, 1)
    rot_cols = lax.dynamic_slice_in_dim(rotations, col_start, n_cols, 2)
    shift_cols = lax.dynamic_slice_in_dim(translations, col_start, n_cols, 1)
    qg = by_head(turn(rot_rows, query_points) + shift_rows[:, None, :], heads)
    kg = by_head(turn(rot_cols, key_points) + shift_cols[:, None, :], heads)
    vg = by_head(turn(rot_cols, value_points) + shift_cols[:, None, :], heads)
    grad_flat = turn(rot_rows, grad_points)
    gg = by_head(grad_flat, heads)
    q = queries.reshape(heads, width, n_rows)
    k = key_vectors.reshape(heads, width, n_cols)
    qsize = width + 3 * qpoints
    nq = 32
    nv = width + 3 * vpoints
    nvp = 48
    c3 = coef[:, None, None]
    q_square = jnp.sum(qg * qg, axis=1, keepdims=True)
    k_square = jnp.sum(kg * kg, axis=1, keepdims=True)
    qcat = pad_to(
        jnp.concatenate(
            [
                logit_scale * inner_scale * q,
                2.0 * c3 * qg,
                jnp.broadcast_to(-c3, (heads, 1, n_rows)),
                -c3 * q_square,
            ],
            axis=1,
        ),
        nq, 128,
    )
    kcat = pad_to(
        jnp.concatenate([k, kg, k_square, jnp.ones((heads, 1, n_cols), F32)], axis=1), nq, n_cols
    )
    gcat = pad_to(
        jnp.concatenate([grad_output.reshape(heads, width, n_rows), gg], axis=1), nvp, 128
    )
    vcat = pad_to(
        jnp.concatenate([values.reshape(heads, width, n_cols), vg], axis=1), nvp, n_cols
    )
    wq = pad_to(
        jnp.concatenate(
            [
                jnp.zeros((heads, width, n_rows), F32), -2.0 * qg,
                jnp.ones((heads, 1, n_rows), F32), q_square,
            ],
            axis=1,
        ),
        nq, n_rows,
    )
    wq = wq.reshape(heads // 4, 4 * nq, n_rows).transpose(0, 2, 1)
    w_t = jnp.pad(bias_weight.T, ((0, PAD - heads), (0, 0)))
    scaled = logit_scale * w_t.astype(F32)
    gpair = jnp.pad(grad_pair, ((0, 0), (0, PAD - heads), (0, 0)))

    vm = pl.BlockSpec(memory_space=pltpu.VMEM)
    big = (heads, n_rows, n_cols)
    flat = (heads * n_rows, n_cols)
    dma = pltpu.SemaphoreType.DMA
    pair_grad, kf, qf, wr = pl.pallas_call(
        functools.partial(mega_kernel, heads, n_rows, n_cols, logit_scale),
        in_specs=[
            pl.BlockSpec(memory_space=pltpu.SMEM),
            pl.BlockSpec(memory_space=pl.ANY),
            *[vm] * 8,
        ],
        out_specs=[vm] * 4,
        out_shape=[
            jax.ShapeDtypeStruct(pair_rep.shape, BF16),
            jax.ShapeDtypeStruct((7, 8, 128), F32),
            jax.ShapeDtypeStruct((6, 8, 128), F32),
            jax.ShapeDtypeStruct((PAD, 128), F32),
        ],
        scratch_shapes=[
            pltpu.VMEM(pair_rep.shape, BF16),
            pltpu.VMEM(big, F32),
            pltpu.VMEM(big, F32),
            *[pltpu.VMEM((n_rows * STRIDE, 128), F32)] * 4,
            *[pltpu.VMEM(flat, BF16)] * 4,
            pltpu.VMEM((3, 256, 256), BF16),
            pltpu.VMEM((4, 288, 256), BF16),
            pltpu.VMEM((32, 128), F32),
            pltpu.VMEM((32, 128), F32),
            pltpu.VMEM((32, 128), F32),
            pltpu.VMEM((3, 32, 128), F32),
            pltpu.VMEM((7, CORES, ZL * YN, 8, 128), F32),
            pltpu.VMEM((7, ZL * YN, 8, 128), F32),
            pltpu.VMEM((YN, 7, ZL, 8, 128), F32),
            pltpu.VMEM((YN - 1, 7, ZL, 8, 128), F32),
            pltpu.VMEM((ZL, 7, 8, 128), F32),
            pltpu.VMEM((ZL - 1, 7, 8, 128), F32),
            pltpu.VMEM((XN, ZH, 6, 8, 128), F32),
            pltpu.VMEM((XN - 1, ZH, 6, 8, 128), F32),
            pltpu.VMEM((ZH, 6, 8, 128), F32),
            pltpu.VMEM((6, 8, 128), F32),
            pltpu.VMEM((PAD, 128), F32),
            pltpu.VMEM((YN, PAD, 128), F32),
            pltpu.VMEM((XN, PAD, 128), F32),
            pltpu.VMEM((ZL * ZH, PAD, 128), F32),
            pltpu.VMEM((4, PAD, 128), F32),
            dma((4,)),
            dma((4,)), dma((4,)),
            dma((7,)), dma((7,)),
            dma((3, 7)), dma((3, 7)),
            dma((3,)), dma((3,)),
            dma((4,)), dma((4,)),
            dma((14,)), dma((14,)),
        ],
        compiler_params=pltpu.CompilerParams(
            collective_id=0, has_side_effects=True, vmem_limit_bytes=VMEM_LIMIT
        ),
        name="mega",
    )(residue_count, pair_rep, w_t, scaled, gpair, qcat, kcat, gcat, vcat, wq)

    weight_total = wr[:heads].T
    distance_total = jnp.sum(wr[heads : heads + 3].reshape(heads, nq), axis=1)
    head_weight_grad = (
        distance_total * (-0.5 * logit_scale * point_scale) * jax.nn.sigmoid(head_weight)
    )
    share = 8
    ksum = kf[:3].reshape(3, share, 4, nq).transpose(0, 2, 3, 1).reshape(heads, nq, share)
    vsum = (
        kf[3:, :, :120].reshape(4, share, 3, nv).transpose(0, 2, 3, 1).reshape(heads, nv, share)
    )
    qsum = qf[:3].reshape(3, share, 4, nq).transpose(0, 2, 3, 1).reshape(heads, nq, share)
    osum = qf[3:].reshape(3, share, 4, nq).transpose(0, 2, 3, 1).reshape(heads, nq, share)

    start = lax.axis_index("col") * share
    own_rows = lambda x: lax.dynamic_slice_in_dim(x, start, share, x.ndim - 1)
    rot_own = own_rows(rot_rows)
    shift_own = own_rows(shift_rows)
    query_grad = (logit_scale * inner_scale * qsum[:, :width]).reshape(heads * width, share)
    dqg = by_axis(
        -2.0 * c3 * (own_rows(qg) * qsum[:, qsize + 1][:, None] - qsum[:, width:qsize])
    )
    point_out = by_axis(osum[:, : nv - width])
    query_point_grad = turn_back(rot_own, dqg)
    cotan_own = own_rows(grad_points)
    out_part = jnp.sum((point_out - shift_own[:, None, :])[:, None] * cotan_own[None], axis=2)
    out_part = jnp.concatenate(
        [out_part, -jnp.sum(own_rows(grad_flat), axis=1)[:, None, :]], axis=1
    )
    query_frame_grad = frame_terms(dqg, own_rows(query_points)) + out_part

    kstart = lax.axis_index("row") * share
    own_cols = lambda x: lax.dynamic_slice_in_dim(x, kstart, share, x.ndim - 1)
    rot_keys = own_cols(rot_cols)
    key_grad = ksum[:, :width].reshape(heads * width, share)
    value_grad = vsum[:, :width].reshape(heads * width, share)
    dkg = by_axis(ksum[:, width:qsize] + 2.0 * own_cols(kg) * ksum[:, qsize][:, None])
    dvg = by_axis(vsum[:, width:])
    key_point_grad = turn_back(rot_keys, dkg)
    value_point_grad = turn_back(rot_keys, dvg)
    key_frame_grad = frame_terms(dkg, own_cols(key_points)) + frame_terms(
        dvg, own_cols(value_points)
    )
    return (
        pair_grad, query_grad, query_point_grad, query_frame_grad, key_grad, value_grad,
        key_point_grad, value_point_grad, key_frame_grad, weight_total, head_weight_grad,
    )


def solution(mesh):
    return jax.shard_map(
        per_device,
        mesh=mesh,
        in_specs=(
            P("row", "col", None),
            P(),
            P(),
            P(None, "row"),
            P(None, "col"),
            P(None, "col"),
            P(None, None, "row"),
            P(None, None, "col"),
            P(None, None, "col"),
            P(),
            P(),
            P(),
            P(None, "row"),
            P(None, None, "row"),
            P("row", None, None),
        ),
        out_specs=(
            P("row", "col", None),
            P(None, ("row", "col")),
            P(None, None, ("row", "col")),
            P(None, None, ("row", "col")),
            P(None, ("col", "row")),
            P(None, ("col", "row")),
            P(None, None, ("col", "row")),
            P(None, None, ("col", "row")),
            P(None, None, ("col", "row")),
            P(),
            P(),
        ),
        check_vma=False,
    )
```

time: 377 us -> 69.3 us (0.18)
  waiting for transfers between devices: 170 us -> 0 us
  Pallas kernels: 152 us -> 37.1 us
  between operations: 17.2 us -> 1.85 us
  other arithmetic: 15.8 us -> 10.7 us
    unnamed x4 -> x0, waiting for transfers between devices: 170 us -> none
    pallas_call x5 -> x1, Pallas kernels: 152 us -> 37.1 us  [per_device(): pl.pallas_call(functools.partial(mega_kernel, heads, n_rows, n_cols, logi...]
    unnamed x27 -> x19, local copies, waits for them, and re-layouts: 9.21 us -> 9.06 us
  transfers between devices with their start and end apart: 2 -> 0, of which waited for: 1 -> 0; matrix products, arithmetic and copies ran while one was open for 3% -> 0% of each run, Pallas kernels for 28% -> 0%
where the time goes in v1:
time: 69.3 us; the launch traced here: 68.7 us
  Pallas kernels  37.1 us (54%)
  local copies, waits for them, and re-layouts  18.9 us (27%)
  other arithmetic  10.7 us (15%)
  between operations  1.85 us (3%)
    pallas_call x1, Pallas kernels, per_device(): pl.pallas_call(functools.partial(mega_kernel, heads, n_rows, n_cols, logi...  37.1 us
    unnamed x19, local copies, waits for them, and re-layouts  9.06 us
    reduce_sum x4, other arithmetic, turn(): return jnp.sum(rotation[:, :, None, :] * local[None], axis=1)  3.01 us
    dynamic_slice x5, local copies, waits for them, and re-layouts, per_device(): own_cols = lambda x: lax.dynamic_slice_in_dim(x, kstart, share, x.ndim - 1)  2.08 us
    reduce_sum x2, other arithmetic, frame_terms(): rotation_part = jnp.sum(grad_global[:, None] * local[None], axis=2)  1.46 us

profile of v1, /device:TPU:1, one launch (start us, length us, event | category | flops | bytes accessed | tf_op | source)
XLA Modules:
  0.0 68.7 jit_solution(11677387971002558701)
XLA Ops:
  1.4 0.1 pad.45.clone
  1.5 0.1 pad.54.clone
  1.6 0.7 broadcast_multiply_fusion.4
  2.3 0.1 constant_dynamic-slice_fusion.9
  2.3 0.1 constant_dynamic-slice_fusion.4
  2.4 0.7 %pad.28.w_t = bf16[16,128]{1,0:T(8,128)(2,1)S(1)} pad(bf16[12,128]{1,0:T(8,128)(2,1)} %bitcast.117, bf16[]{:T(256)} %constant.66.clone.1), padding=0_4x0_0 | pad | bytes 7170 | tf_op jit(solution)/shard_map/jit(_pad)/pad | solution.py:494
  3.1 0.8 %constant_dynamic-slice_fusion.10 = f32[3,3,64]{2,1,0:T(4,128)S(1)} fusion(f32[3,3,2048]{2,1,0:T(4,128)} %param.24, s32[]{:T(128)S(6)} %select_n.35), kind=kLoop, calls=%fused_computation.57 | loop fusion | bytes 4612 | tf_op jit(solution)/shard_map/dynamic_slice | solution.py:444
  3.9 0.7 %convert_multiply_fusion.scaled = f32[16,128]{1,0:T(8,128)S(1)} fusion(bf16[12,128]{1,0:T(8,128)(2,1)} %bitcast.118), kind=kLoop, calls=%fused_computation.42 | loop fusion | flops 4096 | bytes 11264 | tf_op jit(solution)/shard_map/mul | solution.py:495
  4.6 0.9 %constant_dynamic-slice_fusion.2 = (f32[3,3,8]{2,1,0:T(4,128)S(1)}, f32[3,3,8]{2,1,0:T(4,128)S(1)}) fusion(f32[3,3,2048]{2,1,0:T(4,128)} %param.24, s32[]{:T(128)S(6)} %dynamic_slice.60, s32[]{:T(128)S(6)} %dynamic_slice.53), kind=kLoop, calls=%fused_computation.49 | loop fusion | bytes 1160 | tf_op jit(solution)/shard_map/dynamic_slice | solution.py:588
  5.5 0.7 %constant_dynamic-slice_fusion.8 = f32[3,3,256]{2,1,0:T(4,128)S(1)} fusion(f32[3,3,2048]{2,1,0:T(4,128)} %param.24, s32[]{:T(128)S(6)} %select_n.36), kind=kLoop, calls=%fused_computation.55 | loop fusion | bytes 18436 | tf_op jit(solution)/shard_map/dynamic_slice | solution.py:446
  6.2 0.8 %broadcast_multiply_fusion.2 = f32[192,64]{0,1:T(8,128)S(1)} fusion(f32[192,64]{0,1:T(8,128)} %param.18), kind=kLoop, calls=%fused_computation.37 | loop fusion | flops 12288 | bytes 98304 | tf_op jit(solution)/shard_map/mul | solution.py:465
  7.1 0.1 copy.150
  7.2 0.9 %multiply_reduce_fusion.3 = f32[3,48,64]{2,1,0:T(8,128)S(1)} fusion(f32[3,48,64]{2,1,0:T(8,128)} %param.21, f32[3,3,64]{2,1,0:T(4,128)S(1)} %constant_dynamic-slice_fusion.10), kind=kLoop, calls=%fused_computation.12 | loop fusion | flops 46080 | bytes 76032 | tf_op jit(solution)/shard_map/reduce_sum | solution.py:402
  8.2 0.1 broadcast_multiply_fusion.3
  8.3 1.0 %constant_dynamic-slice_fusion.5 = f32[3,48,8]{2,1,0:T(8,128)S(1)} fusion(f32[3,48,64]{2,1,0:T(8,128)} %param.21, s32[]{:T(128)S(6)} %select_n.37), kind=kLoop, calls=%fused_computation.52 | loop fusion | bytes 9220 | tf_op jit(solution)/shard_map/dynamic_slice | solution.py:571
  9.3 1.0 %constant_dynamic-slice_fusion.1 = f32[3,48,8]{2,1,0:T(8,128)S(1)} fusion(f32[3,48,256]{2,1,0:T(8,128)} %param.22, s32[]{:T(128)S(6)} %select_n.40), kind=kLoop, calls=%fused_computation.48 | loop fusion | bytes 9220 | tf_op jit(solution)/shard_map/dynamic_slice | solution.py:588
  10.4 1.1 %multiply_reduce_fusion.2 = f32[3,96,64]{1,2,0:T(8,128)S(1)} fusion(f32[3,96,64]{1,2,0:T(8,128)} %param.28, f32[3,3,64]{2,1,0:T(4,128)S(1)} %constant_dynamic-slice_fusion.10), kind=kLoop, calls=%fused_computation.11 | loop fusion | flops 92160 | bytes 149760 | tf_op jit(solution)/shard_map/reduce_sum | solution.py:402
  11.5 0.8 %dynamic-slice_reduce_fusion = (f32[3,8]{1,0:T(4,128)S(1)}, f32[3,96,8]{1,2,0:T(8,128)S(1)}) fusion(f32[3,96,64]{1,2,0:T(8,128)S(1)} %multiply_reduce_fusion.2, s32[]{:T(128)S(6)} %select_n.37, f32[3,96,64]{1,2,0:T(8,128)} %param.28), kind=kLoop, calls=%fused_computation.38 | loop fusion | flops 2280 | bytes 27748 | tf_op jit(solution)/shard_map/reduce_sum | solution.py:583
  12.3 0.1 copy.154
  12.5 0.9 %copy.153 = f32[192,64]{1,0:T(8,128)S(1)} copy(f32[192,64]{0,1:T(8,128)} %param.27) | data formatting | bytes 98304 | tf_op args[12]
  13.4 1.0 %multiply_reduce_fusion.1 = f32[3,48,256]{2,1,0:T(8,128)S(1)} fusion(f32[3,48,256]{2,1,0:T(8,128)} %param.22, f32[3,3,256]{2,1,0:T(4,128)S(1)} %constant_dynamic-slice_fusion.8), kind=kLoop, calls=%fused_computation.3 | loop fusion | flops 184320 | bytes 304128 | tf_op jit(solution)/shard_map/reduce_sum | solution.py:402
  14.6 0.1 constant_dynamic-slice_fusion
  14.8 0.1 broadcast_multiply_fusion
  15.0 0.1 pad_maximum_fusion
  15.1 0.1 copy.157
  15.2 0.1 copy.149
  15.6 0.1 maximum_maximum_fusion
  15.8 37.1 %mega.1 = (bf16[64,256,128]{2,1,0:T(8,128)(2,1)S(1)}, f32[7,8,128]{2,1,0:T(8,128)S(1)}, f32[6,8,128]{2,1,0:T(8,128)S(1)}, f32[16,128]{1,0:T(8,128)S(1)}) custom-call(s32[1]{0:T(128)S(6)} %copy.198.rc, bf16[64,256,128]{2,1,0:T(8,128)(2,1)} %pair_hbm.1, bf16[16,128]{1,0:T(8,128)(2,1)S(1)} %pad.28.w_t, f32[16,128]{1,0:T(8,128)S(1)} %convert_multiply_fusion.scaled, ...), custom_call_target="tpu_custom_call" | custom-call | tf_op jit(solution)/shard_map/mega/pallas_call | solution.py:502
  52.9 1.9 %copy-done.1 = bf16[64,256,128]{2,1,0:T(8,128)(2,1)} copy-done((bf16[64,256,128]{2,1,0:T(8,128)(2,1)}, bf16[64,256,128]{2,1,0:T(8,128)(2,1)S(1)}, u32[]{:S(2)}) %copy-start.1) | copy-done | bytes 4194328
  54.9 0.6 slice_bitcast_fusion
  55.5 0.1 reshape.203
  55.5 0.1 reduce_sum.191
  55.7 0.5 divide_multiply_fusion
  56.2 0.1 reshape.191
  56.3 0.1 copy.167
  56.4 0.1 reshape.198
  56.5 0.1 slice.68
  56.6 0.1 copy.179
  56.8 0.1 reduce_sum.190
  56.9 0.7 reshape.200
  57.6 0.2 copy.180
  57.8 0.1 mul.326
  57.9 0.7 %multiply_reduce_fusion.6 = (f32[3,3,8]{2,1,0:T(4,128)S(1)}, f32[3,96,8]{1,2,0:T(8,128)}) fusion(f32[3,96,8]{1,2,0:T(8,128)S(1)} %copy.183, f32[3,96,8]{1,2,0:T(8,128)S(1)} %mul.326, f32[3,3,8]{2,1,0:T(4,128)S(1)} %get-tuple-element.86), kind=kLoop, calls=%fused_computation.30 | loop fusion | flops 25272 | bytes 28224 | tf_op jit(solution)/shard_map/reduce_sum | solution.py:410
  58.6 0.2 copy.168
  58.8 0.1 reshape.194
  59.0 0.1 multiply_reduce_fusion.10
  59.1 0.1 copy.189
  59.3 0.1 slice_add_fusion
  59.4 0.1 copy.176
  59.6 0.7 copy.186
  60.2 0.1 reduce_sum.188
  60.3 0.1 copy.177
  60.5 0.1 copy.178
  60.5 0.1 copy.187
  60.7 0.1 fusion.1
  60.9 0.1 copy.161
  61.0 0.7 copy.185
  61.7 0.1 reduce_sum.182
  61.8 0.1 copy.162
  61.9 0.1 copy.163
  62.0 0.8 %multiply_reduce_fusion.7 = (f32[3,3,8]{2,1,0:T(4,128)S(1)}, f32[3,48,8]{1,2,0:T(8,128)}, f32[3,48,8]{1,2,0:T(8,128)}, f32[3,3,8]{2,1,0:T(4,128)S(1)}) fusion(f32[3,48,8]{1,2,0:T(8,128)S(1)} %copy.181, f32[3,48,8]{1,2,0:T(8,128)S(1)} %copy.178, f32[3,3,8]{2,1,0:T(4,128)S(1)} %get-tuple-element.86, f32[3,3,8]{2,1,0:T(4,128)S(1)} %get-tuple-element.87, ...), kind=kLoop, calls=%fused_computation.31 | loop fusion | flops 25200 | bytes 28800 | tf_op jit(solution)/shard_map/reduce_sum | solution.py:410
  62.7 0.6 maximum_add_fusion
  63.3 0.6 maximum_add_fusion.1
  64.0 4.7 %copy.199 = bf16[64,256,128]{2,1,0:T(8,128)(2,1)} copy(bf16[64,256,128]{2,1,0:T(8,128)(2,1)} %copy-done.1) | data formatting | bytes 8388608
  (58 shorter events, 1.1 us)
Async XLA Ops:
  0.6 1.6 %copy-start = (f32[3,2048]{1,0:T(4,128)S(1)}, f32[3,2048]{1,0:T(4,128)}, u32[]{:S(2)}) copy-start(f32[3,2048]{1,0:T(4,128)} %param.25) | copy-start | bytes 73732
  0.7 14.0 %copy-start.2 = (f32[3,96,256]{2,1,0:T(8,128)S(1)}, f32[3,96,256]{2,1,0:T(8,128)}, u32[]{:S(2)}) copy-start(f32[3,96,256]{2,1,0:T(8,128)} %param.23) | copy-start | bytes 884740
  0.7 14.6 %copy-start.3 = (bf16[64,12,128]{2,0,1:T(8,128)(2,1)S(1)}, bf16[64,12,128]{2,0,1:T(8,128)(2,1)}, u32[]{:S(2)}) copy-start(bf16[64,12,128]{2,0,1:T(8,128)(2,1)} %param.29) | copy-start | bytes 589828
  8.1 7.5 %copy-start.5 = (f32[192,256]{1,0:T(8,128)S(1)}, f32[192,256]{1,0:T(8,128)}, u32[]{:S(2)}) copy-start(f32[192,256]{1,0:T(8,128)} %param.20) | copy-start | bytes 589828
  11.5 4.2 %copy-start.4 = (f32[192,256]{1,0:T(8,128)S(1)}, f32[192,256]{1,0:T(8,128)}, u32[]{:S(2)}) copy-start(f32[192,256]{1,0:T(8,128)} %param.19) | copy-start | bytes 589828
  15.6 40.1 %copy-start.6 = (f32[12]{0:T(128)S(1)}, f32[12]{0:T(128)}, u32[]{:S(2)}) copy-start(f32[12]{0:T(128)} %param.17) | copy-start | bytes 148
  52.9 1.9 %copy-start.1 = (bf16[64,256,128]{2,1,0:T(8,128)(2,1)}, bf16[64,256,128]{2,1,0:T(8,128)(2,1)S(1)}, u32[]{:S(2)}) copy-start(bf16[64,256,128]{2,1,0:T(8,128)(2,1)S(1)} %get-tuple-element.109) | copy-start | bytes 12582916

commit v2 on v1

--- a/solution.py
+++ b/solution.py
@@ -11,7 +11,7 @@
 F32 = jnp.float32
 BF16 = jnp.bfloat16
 PAD = 16
-VMEM_LIMIT = 48 * 1024 * 1024
+VMEM_LIMIT = 62700000
 ZL, YN, CORES = 4, 4, 2
 XN, ZH = 4, 2
 STRIDE = 40
@@ -64,17 +64,43 @@
     return copy
 
 
+def group_mask(width, point, spread):
+    row = lax.broadcasted_iota(jnp.int32, (128, 256), 0)
+    lane = lane_of((128, 256))
+    if width:
+        body = (row - width * PAD) % (width * point)
+        head = jnp.where(row < width * PAD, row // PAD, body // point)
+    else:
+        head = (row % 32) // point
+    return head, lane // spread
+
+
+def spread_heads(left, mask):
+    left = jnp.concatenate([left, jnp.zeros_like(left)], 1)
+    left = left + pltpu.roll(left, 64, 1)
+    return jnp.where(mask, jnp.concatenate([left, left], 1), 0.0)
+
+
+def soft(head_weight):
+    return jnp.maximum(head_weight, 0.0) + jnp.log(1.0 + jnp.exp(-jnp.abs(head_weight)))
+
+
 def mega_kernel(
-    heads, n_rows, n_cols, scale,
-    rc, pair_hbm, w_t, scaled, gpair, qcat, kcat, gcat, vcat, wq,
-    pg_out, kf_out, qf_out, wr_out,
+    heads, n_rows, n_cols, scale, inner, coef_scale,
+    rc, pair_hbm, *refs,
+):
+    sources, refs = refs[:13], refs[13:]
+    pg_out, kf_out, qf_out, wr_out = refs[:4]
+    staged, refs = refs[4:17], refs[17:]
+    bw, hw, gp_t, qt, kt, vt, qp, kp, vp, rot, shift, got, gpt = staged
+    (
     pair, lbase, dbase, fb0, fb1, rd0, rd1, a_hi, a_lo, d_hi, d_lo,
-    qb, gb, stat, stat_z, stat_m, stat_x,
+    wgf, wgb, qc, kc, wq, stat, stat_z, stat_m, stat_x,
     ks, ks_rx, sy, sy_rx, sz, sz_rx, qs, qs_rx, qz, qz_rx,
     ar_c, ar_y, ar_x, ar_z, ar_s,
-    pair_sem, s_send, s_recv, k_send, k_recv, y_send, y_recv, z_send, z_recv,
+    pair_sem, in_sem, s_send, s_recv, k_send, k_recv, y_send, y_recv, z_send, z_recv,
     q_send, q_recv, a_send, a_recv,
-):
+    ) = refs
     rw = lax.axis_index("row")
     cl = lax.axis_index("col")
     core = lax.rem(rw, CORES)
@@ -104,6 +130,10 @@
             barrier, inc=1, device_id={"row": peer[0], "col": peer[1]}, device_id_type=MESH
         )
 
+    incoming = []
+    for n, (source, target) in enumerate(zip(sources, staged)):
+        incoming.append(pltpu.make_async_copy(source, target, in_sem.at[n]))
+        incoming[-1].start()
     parts = 4
     rows_per = n_rows // parts
     loads = []
@@ -113,16 +143,78 @@
         load.start()
         loads.append(load)
 
+    wgf[...] = jnp.zeros_like(wgf)
+    for copy in incoming:
+        copy.wait()
+    w_all = bw[...].astype(F32)
+    w_t = jnp.concatenate([w_all, jnp.zeros((PAD - heads, 128), F32)], 0)
     for h in range(heads):
-        q0, q1, q2 = split3(qcat[h][:, :n_rows])
-        k0, k1, k2 = split3(kcat[h])
+        wgf[pl.ds(PAD + h, n_rows, stride=STRIDE), :] = gp_t[h].astype(F32)
+    w_bf = w_t.astype(BF16)
+    for r in range(n_rows):
+        wgb[r, :PAD, :] = w_bf
+        wgb[r, PAD:, :] = wgf[r * STRIDE + PAD : r * STRIDE + 2 * PAD, :].astype(BF16)
+
+    row_block = pl.multiple_of((rw // 2) * 128, 128)
+    col_block = pl.multiple_of(cl * n_cols, 128)
+
+    def row_vec(ref, *index):
+        v = ref[index + (pl.ds(row_block, 128),)]
+        return jnp.where(core == 1, pltpu.roll(v, 64, 1), v)[:, :n_rows]
+
+    rot_q = [[row_vec(rot, x, pl.ds(y, 1)) for y in range(3)] for x in range(3)]
+    rot_k = [
+        [rot[x, pl.ds(y, 1), pl.ds(col_block, n_cols)] for y in range(3)] for x in range(3)
+    ]
+    apply = lambda m, p: [m[x][0] * p[0] + m[x][1] * p[1] + m[x][2] * p[2] for x in range(3)]
+    add_shift = lambda g, t: [g[x] + t[x] for x in range(3)]
+    qg = add_shift(
+        apply(rot_q, [qp[y] for y in range(3)]),
+        [row_vec(shift, pl.ds(x, 1)) for x in range(3)],
+    )
+    shift_k = [shift[pl.ds(x, 1), pl.ds(col_block, n_cols)] for x in range(3)]
+    kg = add_shift(apply(rot_k, [kp[y] for y in range(3)]), shift_k)
+    vg = add_shift(apply(rot_k, [vp[y] for y in range(3)]), shift_k)
+    gg = apply(rot_q, [gpt[y].T for y in range(3)])
+    tall = lambda ref: jnp.concatenate([ref[:, :128].T, ref[:, 128:].T], 0)
+    q_all = tall(qt)
+    g_all = tall(got)
+    q_sq = qg[0] * qg[0] + qg[1] * qg[1] + qg[2] * qg[2]
+    k_sq = kg[0] * kg[0] + kg[1] * kg[1] + kg[2] * kg[2]
+    size = q_sq.shape[0]
+    back = lambda x, n: pltpu.roll(x, size - n, 0)
+    q_sq = q_sq + back(q_sq, 1) + back(q_sq, 2) + back(q_sq, 3)
+    k_sq = k_sq + pltpu.roll(k_sq, 1, 0) + pltpu.roll(k_sq, 2, 0) + pltpu.roll(k_sq, 3, 0)
+    coef = coef_scale * soft(hw[...])
+
+    for h in range(heads):
+        c = coef[:, h : h + 1]
+        qc[h, :PAD, :] = (scale * inner) * q_all[PAD * h : PAD * h + PAD]
+        kc[h, :PAD, :] = kt[PAD * h : PAD * h + PAD, :]
+        for x in range(3):
+            qc[h, PAD + 4 * x : PAD + 4 * x + 4, :] = (2.0 * c) * qg[x][4 * h : 4 * h + 4]
+            kc[h, PAD + 4 * x : PAD + 4 * x + 4, :] = kg[x][4 * h : 4 * h + 4]
+        qc[h, 28:29, :] = jnp.broadcast_to(-c, (1, n_rows))
+        qc[h, 29:30, :] = -c * q_sq[4 * h : 4 * h + 1]
+        qc[h, 30:32, :] = jnp.zeros((2, n_rows), F32)
+        kc[h, 28:29, :] = k_sq[4 * h + 3 : 4 * h + 4]
+        kc[h, 29:30, :] = jnp.ones((1, n_cols), F32)
+        kc[h, 30:32, :] = jnp.zeros((2, n_cols), F32)
+
+    def point_rows(head, points, h):
+        body = [points[x][8 * h : 8 * h + 8] for x in range(3)]
+        return jnp.concatenate([head] + body + [jnp.zeros_like(body[0])], 0)
+
+    for h in range(heads):
+        q0, q1, q2 = split3(qc[h])
+        k0, k1, k2 = split3(kc[h])
         lbase[h] = dot(
             jnp.concatenate([q0, q0, q1, q0, q2, q1], 0),
             jnp.concatenate([k0, k1, k0, k2, k0, k1], 0),
             TN,
         )
-        g0, g1 = split2(gcat[h][:, :n_rows])
-        v0, v1 = split2(vcat[h])
+        g0, g1 = split2(point_rows(g_all[PAD * h : PAD * h + PAD], gg, h))
+        v0, v1 = split2(point_rows(vt[PAD * h : PAD * h + PAD, :], vg, h))
         dbase[h] = dot(
             jnp.concatenate([g0, g0, g1], 0), jnp.concatenate([v0, v1, v0], 0), TN
         )
@@ -132,8 +224,7 @@
 
         for i in range(rows_per):
             r = p * rows_per + i
-            w = jnp.concatenate([w_t[...], gpair[r]], 0)
-            res = dot(w, pair[r], NT)
+            res = dot(wgb[r], pair[r], NT)
             fb0[r * STRIDE : r * STRIDE + 2 * PAD, :] = res[:, :128]
             fb1[r * STRIDE : r * STRIDE + 2 * PAD, :] = res[:, 128:]
 
@@ -165,25 +256,45 @@
 
     rd0[...] = jnp.zeros_like(rd0)
     rd1[...] = jnp.zeros_like(rd1)
-    qb[...] = jnp.zeros_like(qb)
-    gb[...] = jnp.zeros_like(gb)
-    for h in range(heads):
-        g, k = h // 4, h % 4
-        x = qcat[h]
-        if k % 2:
-            x = pltpu.roll(x, 64, 1)
-        c0 = 128 * (k // 2)
-        hi, lo = split2(x)
-        qb[g, 32 * k : 32 * k + 32, c0 : c0 + 128] = hi
-        qb[g, 128 + 32 * k : 160 + 32 * k, c0 : c0 + 128] = lo
-        g, k = h // 3, h % 3
-        x = gcat[h]
-        if k % 2:
-            x = pltpu.roll(x, 64, 1)
-        c0 = 128 * (k // 2)
-        hi, lo = split2(x)
-        gb[g, 48 * k : 48 * k + 48, c0 : c0 + 128] = hi
-        gb[g, 144 + 48 * k : 192 + 48 * k, c0 : c0 + 128] = lo
+    key_head, lane64 = group_mask(4, 4, 64)
+    key_mask = key_head == lane64
+    val_head, _ = group_mask(3, 8, 64)
+    val_mask = val_head == lane64
+    sub16 = lax.broadcasted_iota(jnp.int32, (PAD, n_rows), 0) % 4
+    sub16k = lax.broadcasted_iota(jnp.int32, (PAD, n_cols), 0) % 4
+    qb, gb, kb, vb = [], [], [], []
+    for g in range(3):
+        pts = slice(PAD * g, PAD * g + PAD)
+        base = jnp.concatenate(
+            [q_all[64 * g : 64 * g + 64]] + [qg[x][pts] for x in range(3)]
+            + [jnp.ones((PAD, n_rows), F32)], 0
+        )
+        qb.append(split2(spread_heads(base, key_mask)))
+        weights = jnp.concatenate(
+            [jnp.zeros((64, n_rows), F32)] + [-2.0 * qg[x][pts] for x in range(3)]
+            + [jnp.where(sub16 == 0, q_sq[pts], jnp.where(sub16 == 3, 1.0, 0.0))], 0
+        )
+        wq[g] = weights.T
+        base = jnp.concatenate(
+            [kt[64 * g : 64 * g + 64, :]] + [kg[x][pts] for x in range(3)]
+            + [jnp.where(sub16k == 3, k_sq[pts], jnp.where(sub16k == 0, 1.0, 0.0))], 0
+        )
+        kb.append(split2(base))
+        oct_rows = slice(32 * g, 32 * g + 32)
+        base = jnp.concatenate(
+            [vg[x][oct_rows] for x in range(3)] + [jnp.zeros((32, n_cols), F32)], 0
+        )
+        vb.append(split2(base))
+    for g in range(4):
+        pts = slice(24 * g, 24 * g + 24)
+        base = jnp.concatenate(
+            [g_all[48 * g : 48 * g + 48]] + [gg[x][pts] for x in range(3)]
+            + [jnp.zeros((8, n_rows), F32)], 0
+        )
+        gb.append(split2(spread_heads(base, val_mask)))
+    query_masks = [key_head == k for k in range(4)]
+    point_head, _ = group_mask(0, 8, 64)
+    point_masks = [point_head == k for k in range(4)]
 
     def landed(dst, send, recv, peer):
         pltpu.make_async_remote_copy(
@@ -218,16 +329,12 @@
         rd0[pl.ds(PAD + h, n_rows, stride=STRIDE), :] = att[:, :128]
         rd1[pl.ds(PAD + h, n_rows, stride=STRIDE), :] = att[:, 128:]
 
-    def key_group(g, left, hi, lo, first, count, width):
+    def key_group(g, pairs, hi, lo, first, count):
         depth = count * n_rows
         rows = pl.ds(first * n_rows, depth)
-        lanes = count * width
-        left = left[:, :depth]
-        res = dot(left, hi[rows], NN)
-        res = res[:lanes] + res[lanes:] + dot(left[:lanes], lo[rows], NN)
-        if lanes > 128:
-            res = jnp.concatenate([res[width * k : width * k + 40] for k in range(count)], 0)
-            res = jnp.concatenate([res, jnp.zeros((8, n_cols), F32)], 0)
+        left, small = pairs[0][:, :depth], pairs[1][:, :depth]
+        res = dot(jnp.concatenate([left, small], 0), hi[rows], NN)
+        res = res[:128] + res[128:] + dot(left, lo[rows], NN)
         flat = res.T.reshape(ZL * YN, CORES, 8, 128)
         for c in range(CORES):
             ks[g, c] = flat[:, c]
@@ -250,46 +357,39 @@
 
     for h in range(4):
         make_head(h)
-    key_group(0, qb[0], d_hi, d_lo, 0, 4, 32)
-    key_group(3, gb[0], a_hi, a_lo, 0, 3, 48)
+    key_group(0, qb[0], d_hi, d_lo, 0, 4)
+    key_group(3, gb[0], a_hi, a_lo, 0, 3)
     for h in range(4, 8):
         make_head(h)
-    key_group(1, qb[1], d_hi, d_lo, 4, 4, 32)
-    key_group(4, gb[1], a_hi, a_lo, 3, 3, 48)
+    key_group(1, qb[1], d_hi, d_lo, 4, 4)
+    key_group(4, gb[1], a_hi, a_lo, 3, 3)
     y_stage(0)
     y_stage(3)
     for h in range(8, 12):
         make_head(h)
-    key_group(2, qb[2], d_hi, d_lo, 8, 4, 32)
-    key_group(5, gb[2], a_hi, a_lo, 6, 3, 48)
-    key_group(6, gb[3], a_hi, a_lo, 9, 3, 48)
+    key_group(2, qb[2], d_hi, d_lo, 8, 4)
+    key_group(5, gb[2], a_hi, a_lo, 6, 3)
+    key_group(6, gb[3], a_hi, a_lo, 9, 3)
     y_stage(1)
     y_stage(4)
 
-    def query_group(source, first, skip):
-        hi_cat, lo_cat, left_hi, left_lo = [], [], [], []
-        for k in range(4):
-            h = first + k
-            block = source[h]
-            if skip:
-                block = jnp.concatenate([block[PAD:40], jnp.zeros((8, n_cols), F32)], 0)
-            hi, lo = split2(block)
-            zero = lambda n: [jnp.zeros((n, n_cols), BF16)] if n else []
-            hi_cat.append(jnp.concatenate(zero(32 * k) + [hi] + zero(96 - 32 * k), 0))
-            lo_cat.append(jnp.concatenate(zero(32 * k) + [lo] + zero(96 - 32 * k), 0))
-            rows = pl.ds(h * n_rows, n_rows)
-            left_hi.append((a_hi if skip else d_hi)[rows])
-            left_lo.append((a_lo if skip else d_lo)[rows])
-        hi_cat = jnp.concatenate(hi_cat, 1)
-        lo_cat = jnp.concatenate(lo_cat, 1)
-        left_hi = jnp.concatenate(left_hi, 1)
-        left_lo = jnp.concatenate(left_lo, 1)
-        res = dot(jnp.concatenate([left_hi, left_lo], 0), hi_cat, NT)
-        return res[:n_rows] + res[n_rows:] + dot(left_hi, lo_cat, NT)
+    def query_group(pairs, masks, hi, lo, first):
+        blocks = lambda x: jnp.concatenate(
+            [jnp.where(m, x, jnp.zeros_like(x)) for m in masks], 1
+        )
+        lefts = lambda ref: jnp.concatenate(
+            [ref[pl.ds((first + k) * n_rows, n_rows)] for k in range(4)], 1
+        )
+        top = lefts(hi)
+        res = dot(jnp.concatenate([top, lefts(lo)], 0), blocks(pairs[0]), NT)
+        return res[:n_rows] + res[n_rows:] + dot(top, blocks(pairs[1]), NT)
 
     distance = []
     for g in range(6):
-        res = query_group(kcat if g < 3 else vcat, 4 * (g % 3), g >= 3)
+        if g < 3:
+            res = query_group(kb[g], query_masks, d_hi, d_lo, 4 * g)
+        else:
+            res = query_group(vb[g - 3], point_masks, a_hi, a_lo, 4 * (g - 3))
         if g < 3:
             distance.append(jnp.sum(res * wq[g], axis=0, keepdims=True))
         flat = res.reshape(XN, ZH, 8, 128)
@@ -307,26 +407,31 @@
     y_stage(5)
     y_stage(6)
 
-    row_block = lambda r: jnp.concatenate(
+    both_rows = lambda r: jnp.concatenate(
         [rd0[r * STRIDE : r * STRIDE + 2 * PAD, :], rd1[r * STRIDE : r * STRIDE + 2 * PAD, :]], 1
     ).astype(BF16)
     acc = jnp.zeros((PAD, 128), F32)
     for r in range(n_rows):
-        acc = acc + dot(row_block(r)[:PAD], pair[r], NN)
+        acc = acc + dot(both_rows(r)[:PAD], pair[r], NN)
     acc = scale * acc
     sub = lax.broadcasted_iota(jnp.int32, (PAD, 128), 0)
-    for g in range(3):
-        acc = jnp.where(sub == heads + g, distance[g], acc)
+    lane1 = lane_of((1, 128))
+    owner = jnp.where(lane1 < 112, (lane1 % PAD) // 4, (lane1 - 112) // 4)
+    dist_row = jnp.zeros((1, 128), F32)
+    for h in range(heads):
+        part = jnp.sum(jnp.where(owner == h % 4, distance[h // 4], 0.0), axis=1, keepdims=True)
+        dist_row = jnp.where(lane1 == h, part, dist_row)
+    acc = jnp.where(sub == heads, dist_row, acc)
     ar_s[0] = acc
     sends.append(push(ar_s.at[0], ar_c, a_send.at[0], a_recv.at[0], *sibling))
 
-    w_hi, w_lo = split2(scaled[...])
+    w_hi, w_lo = split2(scale * w_t)
 
     def pair_rows(first, count):
         for r in range(first, first + count):
-            a = row_block(r)
+            a = both_rows(r)
             lhs = jnp.concatenate([a, a[:PAD]], 0)
-            rhs = jnp.concatenate([w_hi, gpair[r], w_lo], 0)
+            rhs = jnp.concatenate([w_hi, wgb[r, PAD:, :], w_lo], 0)
             pg_out[r] = dot(lhs, rhs, TN).astype(BF16)
 
     quarter = n_rows // 4
@@ -398,31 +503,120 @@
         copy.wait_send()
 
 
-def turn(rotation, local):
-    return jnp.sum(rotation[:, :, None, :] * local[None], axis=1)
-
-
-def turn_back(rotation, vector):
-    return jnp.sum(rotation[:, :, None, :] * vector[:, None], axis=0)
-
-
-def frame_terms(grad_global, local):
-    rotation_part = jnp.sum(grad_global[:, None] * local[None], axis=2)
-    return jnp.concatenate([rotation_part, jnp.sum(grad_global, axis=1)[:, None, :]], axis=1)
-
-
-def by_head(x, heads):
-    points = x.shape[1] // heads
-    return x.reshape(3, heads, points, -1).transpose(1, 0, 2, 3).reshape(heads, 3 * points, -1)
-
-
-def by_axis(x):
-    heads, rows, m = x.shape
-    return x.reshape(heads, 3, rows // 3, m).transpose(1, 0, 2, 3).reshape(3, heads * rows // 3, m)
-
-
-def pad_to(x, rows, lanes):
-    return jnp.pad(x, ((0, 0), (0, rows - x.shape[1]), (0, lanes - x.shape[2])))
+def finish_kernel(
+    heads, n_rows, scale, inner, coef_scale,
+    pg, kf, qf, wr, hw_hbm, qp_hbm, kp_hbm, vp_hbm, rot_hbm, shift_hbm, gpt_hbm,
+    pg_out, qgrad, qpgrad, qframe, kgrad, vgrad, kpgrad, vpgrad, kframe, weight, head_out,
+    hw, qp, kp, vp, rot, shift, gpt, turned, in_sem, sem,
+):
+    incoming = []
+    sources = (hw_hbm, qp_hbm, kp_hbm, vp_hbm, rot_hbm, shift_hbm, gpt_hbm)
+    for n, (source, target) in enumerate(zip(sources, (hw, qp, kp, vp, rot, shift, gpt))):
+        incoming.append(pltpu.make_async_copy(source, target, in_sem.at[n]))
+        incoming[-1].start()
+    copy = pltpu.make_async_copy(pg, pg_out, sem)
+    copy.start()
+    rw = lax.axis_index("row")
+    cl = lax.axis_index("col")
+    weight[...] = wr[:heads, :]
+    for load in incoming:
+        load.wait()
+    sig = 1.0 / (1.0 + jnp.exp(-hw[...]))
+    head_out[...] = wr[heads : heads + 1, :heads] * (-coef_scale) * sig
+    coef = coef_scale * soft(hw[...])
+
+    def frames(start):
+        block = pl.multiple_of((start // 128) * 128, 128)
+        rows = [rot[x, pl.ds(y, 1), pl.ds(block, 128)] for x in range(3) for y in range(3)]
+        rows += [shift[pl.ds(x, 1), pl.ds(block, 128)] for x in range(3)]
+        rows = jnp.concatenate(rows + [jnp.zeros((4, 128), F32)], 0)
+        turned[:, :PAD] = rows.T
+        own = turned[pl.ds(pl.multiple_of(start % 128, 8), 8), :PAD]
+        entry = lambda k: own[:, k : k + 1]
+        return [[entry(3 * x + y) for y in range(3)] for x in range(3)], [
+            entry(9 + x) for x in range(3)
+        ]
+
+    def local(ref, lanes, offset):
+        out = []
+        for y in range(3):
+            x = ref[y] if lanes is None else ref[y, :, lanes]
+            x = x.T
+            turned[: x.shape[0], : x.shape[1]] = x
+            out.append(turned[pl.ds(pl.multiple_of(offset, 8), 8), : x.shape[1]])
+        return out
+
+    apply = lambda m, p: [m[x][0] * p[0] + m[x][1] * p[1] + m[x][2] * p[2] for x in range(3)]
+    undo = lambda m, v: [m[0][y] * v[0] + m[1][y] * v[1] + m[2][y] * v[2] for y in range(3)]
+    add_all = lambda x: jnp.sum(x, axis=1, keepdims=True)
+    lane8 = lane_of((8, 128))
+
+    def gather(parts, offset, size):
+        return jnp.concatenate([p[:, offset : offset + size] for p in parts], 1)
+
+    c48 = jnp.zeros((1, 128), F32)
+    lane1 = lane_of((1, 128))
+    for h in range(heads):
+        c48 = jnp.where(lane1 // 4 == h, coef[:, h : h + 1], c48)
+    c48 = c48[:, :48]
+
+    def frame_out(ref, entries):
+        tile = jnp.zeros((8, 128), F32)
+        for k, value in enumerate(entries):
+            tile = jnp.where(lane8 == k, value, tile)
+        tile = tile.T
+        for x in range(3):
+            ref[x] = tile[4 * x : 4 * x + 4, :]
+
+    rot_q, shift_q = frames(rw * n_rows + cl * 8)
+    points = local(qp, None, cl * 8)
+    cotan = [gpt[y, pl.ds(pl.multiple_of(cl * 8, 8), 8), :] for y in range(3)]
+    qg = [v + shift_q[x] for x, v in enumerate(apply(rot_q, points))]
+    gg = apply(rot_q, cotan)
+    parts = [qf[g] for g in range(3)]
+    qgrad[...] = (scale * inner) * gather(parts, 0, 64)
+    ones = []
+    for p in parts:
+        v = jnp.where((lane8 >= 112) & (lane8 % 4 == 0), p, 0.0)
+        ones.append(v + pltpu.roll(v, 1, 1) + pltpu.roll(v, 2, 1) + pltpu.roll(v, 3, 1))
+    ones = gather(ones, 112, PAD)
+    dqg = [
+        -2.0 * c48 * (qg[x] * ones - gather(parts, 64 + PAD * x, PAD)) for x in range(3)
+    ]
+    parts = [qf[3 + g] for g in range(3)]
+    opt = [gather(parts, 32 * x, 32) - shift_q[x] for x in range(3)]
+    for y, v in enumerate(undo(rot_q, dqg)):
+        qpgrad[y] = v
+    entries = []
+    for x in range(3):
+        for y in range(3):
+            entries.append(add_all(dqg[x] * points[y]) + add_all(opt[x] * cotan[y]))
+        entries.append(add_all(dqg[x]) - add_all(gg[x]))
+    frame_out(qframe, entries)
+
+    rot_k, shift_k = frames(cl * 256 + rw * 8)
+    lanes = pl.ds(pl.multiple_of((rw // 16) * 128, 128), 128)
+    points = local(kp, lanes, (rw % 16) * 8)
+    vpoints = local(vp, lanes, (rw % 16) * 8)
+    kg = [v + shift_k[x] for x, v in enumerate(apply(rot_k, points))]
+    parts = [kf[g] for g in range(3)]
+    kgrad[...] = (scale * inner) * gather(parts, 0, 64)
+    ones = gather(parts, 112, PAD)
+    dkg = [2.0 * c48 * (gather(parts, 64 + PAD * x, PAD) - kg[x] * ones) for x in range(3)]
+    parts = [kf[3 + g] for g in range(4)]
+    vgrad[...] = gather(parts, 0, 48)
+    dvg = [gather(parts, 48 + 24 * x, 24) for x in range(3)]
+    for y, v in enumerate(undo(rot_k, dkg)):
+        kpgrad[y] = v
+    for y, v in enumerate(undo(rot_k, dvg)):
+        vpgrad[y] = v
+    entries = []
+    for x in range(3):
+        for y in range(3):
+            entries.append(add_all(dkg[x] * points[y]) + add_all(dvg[x] * vpoints[y]))
+        entries.append(add_all(dkg[x]) + add_all(dvg[x]))
+    frame_out(kframe, entries)
+    copy.wait()
 
 
 def per_device(
@@ -432,80 +626,30 @@
     channels, heads = bias_weight.shape
     width = queries.shape[0] // heads
     qpoints = query_points.shape[1] // heads
-    vpoints = value_points.shape[1] // heads
     n_rows = queries.shape[1]
     n_cols = key_vectors.shape[1]
     logit_scale = math.sqrt(1.0 / 3.0)
     point_scale = math.sqrt(2.0 / (9.0 * qpoints))
     inner_scale = 1.0 / math.sqrt(width)
-    coef = 0.5 * logit_scale * point_scale * jax.nn.softplus(head_weight)
-    row_start = lax.axis_index("row") * n_rows
-    col_start = lax.axis_index("col") * n_cols
-    rot_rows = lax.dynamic_slice_in_dim(rotations, row_start, n_rows, 2)
-    shift_rows = lax.dynamic_slice_in_dim(translations, row_start, n_rows, 1)
-    rot_cols = lax.dynamic_slice_in_dim(rotations, col_start, n_cols, 2)
-    shift_cols = lax.dynamic_slice_in_dim(translations, col_start, n_cols, 1)
-    qg = by_head(turn(rot_rows, query_points) + shift_rows[:, None, :], heads)
-    kg = by_head(turn(rot_cols, key_points) + shift_cols[:, None, :], heads)
-    vg = by_head(turn(rot_cols, value_points) + shift_cols[:, None, :], heads)
-    grad_flat = turn(rot_rows, grad_points)
-    gg = by_head(grad_flat, heads)
-    q = queries.reshape(heads, width, n_rows)
-    k = key_vectors.reshape(heads, width, n_cols)
-    qsize = width + 3 * qpoints
-    nq = 32
-    nv = width + 3 * vpoints
-    nvp = 48
-    c3 = coef[:, None, None]
-    q_square = jnp.sum(qg * qg, axis=1, keepdims=True)
-    k_square = jnp.sum(kg * kg, axis=1, keepdims=True)
-    qcat = pad_to(
-        jnp.concatenate(
-            [
-                logit_scale * inner_scale * q,
-                2.0 * c3 * qg,
-                jnp.broadcast_to(-c3, (heads, 1, n_rows)),
-                -c3 * q_square,
-            ],
-            axis=1,
-        ),
-        nq, 128,
-    )
-    kcat = pad_to(
-        jnp.concatenate([k, kg, k_square, jnp.ones((heads, 1, n_cols), F32)], axis=1), nq, n_cols
-    )
-    gcat = pad_to(
-        jnp.concatenate([grad_output.reshape(heads, width, n_rows), gg], axis=1), nvp, 128
-    )
-    vcat = pad_to(
-        jnp.concatenate([values.reshape(heads, width, n_cols), vg], axis=1), nvp, n_cols
-    )
-    wq = pad_to(
-        jnp.concatenate(
-            [
-                jnp.zeros((heads, width, n_rows), F32), -2.0 * qg,
-                jnp.ones((heads, 1, n_rows), F32), q_square,
-            ],
-            axis=1,
-        ),
-        nq, n_rows,
-    )
-    wq = wq.reshape(heads // 4, 4 * nq, n_rows).transpose(0, 2, 1)
-    w_t = jnp.pad(bias_weight.T, ((0, PAD - heads), (0, 0)))
-    scaled = logit_scale * w_t.astype(F32)
-    gpair = jnp.pad(grad_pair, ((0, 0), (0, PAD - heads), (0, 0)))
+    coef_scale = 0.5 * logit_scale * point_scale
+    hw = head_weight.reshape(1, heads)
+    gpt = grad_points.transpose(0, 2, 1)
 
     vm = pl.BlockSpec(memory_space=pltpu.VMEM)
+    hbm = pl.BlockSpec(memory_space=pltpu.HBM)
     big = (heads, n_rows, n_cols)
     flat = (heads * n_rows, n_cols)
     dma = pltpu.SemaphoreType.DMA
-    pair_grad, kf, qf, wr = pl.pallas_call(
-        functools.partial(mega_kernel, heads, n_rows, n_cols, logit_scale),
-        in_specs=[
-            pl.BlockSpec(memory_space=pltpu.SMEM),
-            pl.BlockSpec(memory_space=pl.ANY),
-            *[vm] * 8,
-        ],
+    inputs = (
+        bias_weight.T, hw, grad_pair.transpose(1, 0, 2), queries.T, key_vectors, values,
+        query_points, key_points, value_points, rotations, translations, grad_output.T, gpt,
+    )
+    like = lambda x: pltpu.VMEM(x.shape, x.dtype)
+    pg, kf, qf, wr = pl.pallas_call(
+        functools.partial(
+            mega_kernel, heads, n_rows, n_cols, logit_scale, inner_scale, coef_scale
+        ),
+        in_specs=[pl.BlockSpec(memory_space=pltpu.SMEM), *[hbm] * 14],
         out_specs=[vm] * 4,
         out_shape=[
             jax.ShapeDtypeStruct(pair_rep.shape, BF16),
@@ -514,13 +658,17 @@
             jax.ShapeDtypeStruct((PAD, 128), F32),
         ],
         scratch_shapes=[
+            *[like(x) for x in inputs],
             pltpu.VMEM(pair_rep.shape, BF16),
             pltpu.VMEM(big, F32),
             pltpu.VMEM(big, F32),
             *[pltpu.VMEM((n_rows * STRIDE, 128), F32)] * 4,
             *[pltpu.VMEM(flat, BF16)] * 4,
-            pltpu.VMEM((3, 256, 256), BF16),
-            pltpu.VMEM((4, 288, 256), BF16),
+            pltpu.VMEM((n_rows * STRIDE, 128), F32),
+            pltpu.VMEM((n_rows, 2 * PAD, 128), BF16),
+            pltpu.VMEM((heads, 32, n_rows), F32),
+            pltpu.VMEM((heads, 32, n_cols), F32),
+            pltpu.VMEM((3, n_rows, 128), F32),
             pltpu.VMEM((32, 128), F32),
             pltpu.VMEM((32, 128), F32),
             pltpu.VMEM((32, 128), F32),
@@ -540,7 +688,7 @@
             pltpu.VMEM((XN, PAD, 128), F32),
             pltpu.VMEM((ZL * ZH, PAD, 128), F32),
             pltpu.VMEM((4, PAD, 128), F32),
-            dma((4,)),
+            dma((4,)), dma((13,)),
             dma((4,)), dma((4,)),
             dma((7,)), dma((7,)),
             dma((3, 7)), dma((3, 7)),
@@ -552,53 +700,40 @@
             collective_id=0, has_side_effects=True, vmem_limit_bytes=VMEM_LIMIT
         ),
         name="mega",
-    )(residue_count, pair_rep, w_t, scaled, gpair, qcat, kcat, gcat, vcat, wq)
-
-    weight_total = wr[:heads].T
-    distance_total = jnp.sum(wr[heads : heads + 3].reshape(heads, nq), axis=1)
-    head_weight_grad = (
-        distance_total * (-0.5 * logit_scale * point_scale) * jax.nn.sigmoid(head_weight)
+    )(
+        residue_count, pair_rep, *inputs
     )
     share = 8
-    ksum = kf[:3].reshape(3, share, 4, nq).transpose(0, 2, 3, 1).reshape(heads, nq, share)
-    vsum = (
-        kf[3:, :, :120].reshape(4, share, 3, nv).transpose(0, 2, 3, 1).reshape(heads, nv, share)
-    )
-    qsum = qf[:3].reshape(3, share, 4, nq).transpose(0, 2, 3, 1).reshape(heads, nq, share)
-    osum = qf[3:].reshape(3, share, 4, nq).transpose(0, 2, 3, 1).reshape(heads, nq, share)
-
-    start = lax.axis_index("col") * share
-    own_rows = lambda x: lax.dynamic_slice_in_dim(x, start, share, x.ndim - 1)
-    rot_own = own_rows(rot_rows)
-    shift_own = own_rows(shift_rows)
-    query_grad = (logit_scale * inner_scale * qsum[:, :width]).reshape(heads * width, share)
-    dqg = by_axis(
-        -2.0 * c3 * (own_rows(qg) * qsum[:, qsize + 1][:, None] - qsum[:, width:qsize])
-    )
-    point_out = by_axis(osum[:, : nv - width])
-    query_point_grad = turn_back(rot_own, dqg)
-    cotan_own = own_rows(grad_points)
-    out_part = jnp.sum((point_out - shift_own[:, None, :])[:, None] * cotan_own[None], axis=2)
-    out_part = jnp.concatenate(
-        [out_part, -jnp.sum(own_rows(grad_flat), axis=1)[:, None, :]], axis=1
-    )
-    query_frame_grad = frame_terms(dqg, own_rows(query_points)) + out_part
-
-    kstart = lax.axis_index("row") * share
-    own_cols = lambda x: lax.dynamic_slice_in_dim(x, kstart, share, x.ndim - 1)
-    rot_keys = own_cols(rot_cols)
-    key_grad = ksum[:, :width].reshape(heads * width, share)
-    value_grad = vsum[:, :width].reshape(heads * width, share)
-    dkg = by_axis(ksum[:, width:qsize] + 2.0 * own_cols(kg) * ksum[:, qsize][:, None])
-    dvg = by_axis(vsum[:, width:])
-    key_point_grad = turn_back(rot_keys, dkg)
-    value_point_grad = turn_back(rot_keys, dvg)
-    key_frame_grad = frame_terms(dkg, own_cols(key_points)) + frame_terms(
-        dvg, own_cols(value_points)
-    )
+    late = (hw, query_points, key_points, value_points, rotations, translations, gpt)
+    f32 = lambda *shape: jax.ShapeDtypeStruct(shape, F32)
+    outs = pl.pallas_call(
+        functools.partial(
+            finish_kernel, heads, n_rows, logit_scale, inner_scale, coef_scale
+        ),
+        in_specs=[vm] * 4 + [hbm] * 7,
+        out_specs=[hbm] + [vm] * 10,
+        out_shape=[
+            jax.ShapeDtypeStruct(pair_rep.shape, BF16),
+            f32(share, heads * width),
+            f32(3, share, 48),
+            f32(3, 4, share),
+            f32(share, heads * width),
+            f32(share, heads * width),
+            f32(3, share, 48),
+            f32(3, share, 96),
+            f32(3, 4, share),
+            f32(heads, channels),
+            f32(1, heads),
+        ],
+        scratch_shapes=[*[like(x) for x in late], pltpu.VMEM((128, 128), F32), dma((7,)), dma],
+        compiler_params=pltpu.CompilerParams(vmem_limit_bytes=VMEM_LIMIT),
+        name="finish",
+    )(pg, kf, qf, wr, *late)
+    (pair_grad, qgrad, qpgrad, qframe, kgrad, vgrad, kpgrad, vpgrad, kframe, weight, head) = outs
+    flip = lambda x: x.transpose(0, 2, 1)
     return (
-        pair_grad, query_grad, query_point_grad, query_frame_grad, key_grad, value_grad,
-        key_point_grad, value_point_grad, key_frame_grad, weight_total, head_weight_grad,
+        pair_grad, qgrad.T, flip(qpgrad), qframe, kgrad.T, vgrad.T, flip(kpgrad), flip(vpgrad),
+        kframe, weight.T, head.reshape(heads),
     )
 
 

time: 69.3 us -> 48.2 us (0.70)
  local copies, waits for them, and re-layouts: 18.9 us -> 0 us
  other arithmetic: 10.7 us -> 0 us
  Pallas kernels: 37.1 us -> 46.8 us
    unnamed x19 -> x0, local copies, waits for them, and re-layouts: 9.06 us -> none
    reduce_sum x14 -> x0, other arithmetic: 5.92 us -> none  [the longest x4 3.01 us: turn(): return jnp.sum(rotation[:, :, None, :] * local[None], axis=1)]
    pallas_call x0 -> x1, Pallas kernels: none -> 5.58 us  [per_device(): pl.pallas_call(functools.partial(finish_kernel, heads, n_rows, logit_scal...]
    dynamic_slice x12 -> x0, local copies, waits for them, and re-layouts: 4.75 us -> none  [the longest x5 2.08 us: per_device(): own_cols = lambda x: lax.dynamic_slice_in_dim(x, kstart, share, x.ndim - 1)]
    pallas_call x1, Pallas kernels: 37.1 us -> 41.2 us  [per_device(): pl.pallas_call(functools.partial(mega_kernel, heads, n_rows, n_cols, logi...]
    mul x10 -> x0, other arithmetic: 3.06 us -> none  [the longest x1 0.85 us: per_device(): logit_scale * inner_scale * q]
    reshape x12 -> x0, local copies, waits for them, and re-layouts: 1.52 us -> none  [the longest x1 0.68 us: per_device(): value_grad = vsum[:, :width].reshape(heads * width, share)]
    transpose x8 -> x0, local copies, waits for them, and re-layouts: 1.34 us -> none  [the longest x4 0.71 us: by_axis(): x.reshape(heads, 3, rows // 3, m).transpose(1, 0, 2, 3)]
where the time goes in v2:
time: 48.2 us; the launch traced here: 48.1 us
  Pallas kernels  46.8 us (97%)
  between operations  1.3 us (3%)
    pallas_call x1, Pallas kernels, per_device(): pl.pallas_call(functools.partial(mega_kernel, heads, n_rows, n_cols, logi...  41.2 us
    pallas_call x1, Pallas kernels, per_device(): pl.pallas_call(functools.partial(finish_kernel, heads, n_rows, logit_scal...  5.58 us

profile of v2, /device:TPU:1, one launch (start us, length us, event | category | flops | bytes accessed | tf_op | source)
XLA Modules:
  0.0 48.1 jit_solution(18217401185447133497)
XLA Ops:
  1.3 41.2 %mega.1 = (bf16[64,256,128]{2,1,0:T(8,128)(2,1)}, f32[7,8,128]{2,1,0:T(8,128)}, f32[6,8,128]{2,1,0:T(8,128)}, f32[16,128]{1,0:T(8,128)}) custom-call(s32[1]{0:T(128)S(6)} %copy.26.rc, bf16[64,256,128]{2,1,0:T(8,128)(2,1)} %pair_hbm.1, bf16[12,128]{1,0:T(8,128)(2,1)} %bitcast.19, f32[1,12]{1,0:T(1,128)} %bitcast.20, bf16[12,64,128]{2,1,0:T(8,128)(2,1)} %bitcast.16, ...), custom_call_target="tpu_custom_call" | custom-call | tf_op jit(solution)/shard_map/mega/pallas_call | solution.py:648
  42.5 5.6 %finish.1 = (bf16[64,256,128]{2,1,0:T(8,128)(2,1)}, f32[8,192]{1,0:T(8,128)}, f32[3,8,48]{2,1,0:T(8,128)}, f32[3,4,8]{2,1,0:T(4,128)}, f32[8,192]{1,0:T(8,128)},...) custom-call(bf16[64,256,128]{2,1,0:T(8,128)(2,1)} %get-tuple-element, ...), custom_call_target="tpu_custom_call" | custom-call | tf_op jit(solution)/shard_map/finish/pallas_call | solution.py:709

commit v3 on v2

--- a/solution.py
+++ b/solution.py
@@ -11,7 +11,7 @@
 F32 = jnp.float32
 BF16 = jnp.bfloat16
 PAD = 16
-VMEM_LIMIT = 62700000
+VMEM_LIMIT = 50331648
 ZL, YN, CORES = 4, 4, 2
 XN, ZH = 4, 2
 STRIDE = 40
@@ -120,16 +120,6 @@
         idx = lax.rem(z8 + k, ZL * ZH)
         return (row_of(lax.rem(idx, ZL), yy, core), xx * ZH + idx // ZL)
 
-    everyone = [sibling]
-    everyone += [y_peer(k) for k in range(1, YN)]
-    everyone += [x_peer(k) for k in range(1, XN)]
-    everyone += [ring_peer(k) for k in range(1, ZL * ZH)]
-    barrier = pltpu.get_barrier_semaphore()
-    for peer in everyone:
-        pl.semaphore_signal(
-            barrier, inc=1, device_id={"row": peer[0], "col": peer[1]}, device_id_type=MESH
-        )
-
     incoming = []
     for n, (source, target) in enumerate(zip(sources, staged)):
         incoming.append(pltpu.make_async_copy(source, target, in_sem.at[n]))
@@ -142,6 +132,16 @@
         load = pltpu.make_async_copy(pair_hbm.at[piece], pair.at[piece], pair_sem.at[p])
         load.start()
         loads.append(load)
+
+    everyone = [sibling]
+    everyone += [y_peer(k) for k in range(1, YN)]
+    everyone += [x_peer(k) for k in range(1, XN)]
+    everyone += [ring_peer(k) for k in range(1, ZL * ZH)]
+    barrier = pltpu.get_barrier_semaphore()
+    for peer in everyone:
+        pl.semaphore_signal(
+            barrier, inc=1, device_id={"row": peer[0], "col": peer[1]}, device_id_type=MESH
+        )
 
     wgf[...] = jnp.zeros_like(wgf)
     for copy in incoming:
@@ -342,18 +342,46 @@
             push(ks.at[g, 1 - core], ks_rx.at[g], k_send.at[g], k_recv.at[g], *sibling)
         )
 
+    z_first = (0, 3)
+
+    def order(g):
+        first, second = (y_peer, yy), (z_peer, zl)
+        return (second, first) if g in z_first else (first, second)
+
     def y_stage(g):
         landed(ks_rx.at[g], k_send.at[g], k_recv.at[g], sibling)
         both = (ks[g, core] + ks_rx[g]).reshape(ZL, YN, 8, 128)
-        for y in range(YN):
-            sy[y, g] = both[:, y]
+        peer, place = order(g)[0]
+        for n in range(YN):
+            sy[n, g] = both[n] if g in z_first else both[:, n]
         for k in range(1, YN):
             sends.append(
                 push(
-                    sy.at[lax.rem(yy + k, YN), g], sy_rx.at[k - 1, g],
-                    y_send.at[k - 1, g], y_recv.at[k - 1, g], *y_peer(k)
+                    sy.at[lax.rem(place + k, YN), g], sy_rx.at[k - 1, g],
+                    y_send.at[k - 1, g], y_recv.at[k - 1, g], *peer(k)
                 )
             )
+
+    def z_stage(g):
+        (peer, place), (after, slot) = order(g)
+        for k in range(1, YN):
+            landed(sy_rx.at[k - 1, g], y_send.at[k - 1, g], y_recv.at[k - 1, g], peer(k))
+        mine = sy[place, g] + sy_rx[0, g] + sy_rx[1, g] + sy_rx[2, g]
+        for n in range(ZL):
+            sz[n, g] = mine[n]
+        for k in range(1, ZL):
+            sends.append(
+                push(
+                    sz.at[lax.rem(slot + k, ZL), g], sz_rx.at[k - 1, g],
+                    z_send.at[k - 1, g], z_recv.at[k - 1, g], *after(k)
+                )
+            )
+
+    def last_stage(g):
+        _, (peer, place) = order(g)
+        for k in range(1, ZL):
+            landed(sz_rx.at[k - 1, g], z_send.at[k - 1, g], z_recv.at[k - 1, g], peer(k))
+        kf_out[g] = sz[place, g] + sz_rx[0, g] + sz_rx[1, g] + sz_rx[2, g]
 
     for h in range(4):
         make_head(h)
@@ -439,57 +467,34 @@
 
     landed(ar_c, a_send.at[0], a_recv.at[0], sibling)
     ar_s[1] = ar_s[0] + ar_c[...]
-    ar_y[yy] = ar_s[1]
-    for k in range(1, YN):
-        sends.append(push(ar_s.at[1], ar_y.at[yy], a_send.at[k], a_recv.at[k], *y_peer(k)))
+    ar_x[xx] = ar_s[1]
+    for k in range(1, XN):
+        sends.append(push(ar_s.at[1], ar_x.at[xx], a_send.at[k], a_recv.at[k], *x_peer(k)))
 
     pair_rows(quarter, quarter)
-
+    z_stage(0)
+    z_stage(3)
     for k in range(1, XN):
         landed(qs_rx.at[k - 1], q_send.at[k - 1], q_recv.at[k - 1], x_peer(k))
     qz[...] = qs[xx] + qs_rx[0] + qs_rx[1] + qs_rx[2]
     sends.append(push(qz.at[1 - zh], qz_rx, q_send.at[3], q_recv.at[3], *h_peer))
 
-    for k in range(1, YN):
-        landed(ar_y.at[lax.rem(yy + YN - k, YN)], a_send.at[k], a_recv.at[k], y_peer(k))
-    ar_s[2] = ar_y[0] + ar_y[1] + ar_y[2] + ar_y[3]
-    ar_x[xx] = ar_s[2]
+    pair_rows(2 * quarter, quarter)
+    z_stage(1)
     for k in range(1, XN):
-        sends.append(
-            push(ar_s.at[2], ar_x.at[xx], a_send.at[3 + k], a_recv.at[3 + k], *x_peer(k))
-        )
-
-    for g in (0, 3, 1, 4, 2, 5, 6):
-        for k in range(1, YN):
-            landed(sy_rx.at[k - 1, g], y_send.at[k - 1, g], y_recv.at[k - 1, g], y_peer(k))
-        mine = sy[yy, g] + sy_rx[0, g] + sy_rx[1, g] + sy_rx[2, g]
-        for z in range(ZL):
-            sz[z, g] = mine[z]
-    for k in range(1, ZL):
-        sends.append(
-            push(
-                sz.at[lax.rem(zl + k, ZL)], sz_rx.at[k - 1],
-                z_send.at[k - 1], z_recv.at[k - 1], *z_peer(k)
-            )
-        )
-    pair_rows(2 * quarter, quarter)
-
-    for k in range(1, XN):
-        landed(ar_x.at[lax.rem(xx + XN - k, XN)], a_send.at[3 + k], a_recv.at[3 + k], x_peer(k))
-    ar_s[3] = ar_x[0] + ar_x[1] + ar_x[2] + ar_x[3]
-    ar_z[z8] = ar_s[3]
+        landed(ar_x.at[lax.rem(xx + XN - k, XN)], a_send.at[k], a_recv.at[k], x_peer(k))
+    ar_s[2] = ar_x[0] + ar_x[1] + ar_x[2] + ar_x[3]
+    ar_z[z8] = ar_s[2]
     for k in range(1, ZL * ZH):
         sends.append(
-            push(ar_s.at[3], ar_z.at[z8], a_send.at[6 + k], a_recv.at[6 + k], *ring_peer(k))
+            push(ar_s.at[2], ar_z.at[z8], a_send.at[6 + k], a_recv.at[6 + k], *ring_peer(k))
         )
 
     pair_rows(3 * quarter, quarter)
-
-    for k in range(1, ZL):
-        landed(sz_rx.at[k - 1], z_send.at[k - 1], z_recv.at[k - 1], z_peer(k))
-    kf_out[...] = sz[zl] + sz_rx[0] + sz_rx[1] + sz_rx[2]
-    landed(qz_rx, q_send.at[3], q_recv.at[3], h_peer)
-    qf_out[...] = qz[zh] + qz_rx[...]
+    z_stage(4)
+    z_stage(2)
+    z_stage(5)
+    z_stage(6)
     for k in range(1, ZL * ZH):
         landed(
             ar_z.at[lax.rem(z8 + ZL * ZH - k, ZL * ZH)], a_send.at[6 + k], a_recv.at[6 + k],
@@ -498,7 +503,21 @@
     grand = ar_z[0]
     for k in range(1, ZL * ZH):
         grand = grand + ar_z[k]
-    wr_out[...] = grand
+    ar_s[3] = grand
+    ar_y[yy] = ar_s[3]
+    for k in range(1, YN):
+        sends.append(
+            push(ar_s.at[3], ar_y.at[yy], a_send.at[3 + k], a_recv.at[3 + k], *y_peer(k))
+        )
+    landed(qz_rx, q_send.at[3], q_recv.at[3], h_peer)
+    qf_out[...] = qz[zh] + qz_rx[...]
+    for g in (0, 3, 1, 4, 2, 5, 6):
+        last_stage(g)
+    for k in range(1, YN):
+        landed(
+            ar_y.at[lax.rem(yy + YN - k, YN)], a_send.at[3 + k], a_recv.at[3 + k], y_peer(k)
+        )
+    wr_out[...] = ar_y[0] + ar_y[1] + ar_y[2] + ar_y[3]
     for copy in sends:
         copy.wait_send()
 
@@ -645,6 +664,7 @@
         query_points, key_points, value_points, rotations, translations, grad_output.T, gpt,
     )
     like = lambda x: pltpu.VMEM(x.shape, x.dtype)
+    inputs = tuple(pltpu.with_memory_space_constraint(x, pltpu.HBM) for x in inputs)
     pg, kf, qf, wr = pl.pallas_call(
         functools.partial(
             mega_kernel, heads, n_rows, n_cols, logit_scale, inner_scale, coef_scale
@@ -652,7 +672,7 @@
         in_specs=[pl.BlockSpec(memory_space=pltpu.SMEM), *[hbm] * 14],
         out_specs=[vm] * 4,
         out_shape=[
-            jax.ShapeDtypeStruct(pair_rep.shape, BF16),
+            pltpu.VMEM(pair_rep.shape, BF16),
             jax.ShapeDtypeStruct((7, 8, 128), F32),
             jax.ShapeDtypeStruct((6, 8, 128), F32),
             jax.ShapeDtypeStruct((PAD, 128), F32),
@@ -692,7 +712,7 @@
             dma((4,)), dma((4,)),
             dma((7,)), dma((7,)),
             dma((3, 7)), dma((3, 7)),
-            dma((3,)), dma((3,)),
+            dma((3, 7)), dma((3, 7)),
             dma((4,)), dma((4,)),
             dma((14,)), dma((14,)),
         ],

time: 48.2 us -> 44.7 us (0.927)
  Pallas kernels: 46.8 us -> 43.1 us
    pallas_call x1, Pallas kernels: 5.58 us -> 3.39 us  [per_device(): pl.pallas_call(functools.partial(finish_kernel, heads, n_rows, logit_scal...]
    pallas_call x1, Pallas kernels: 41.2 us -> 39.7 us  [per_device(): pl.pallas_call(functools.partial(mega_kernel, heads, n_rows, n_cols, logi...]
where the time goes in v3:
time: 44.7 us; the launch traced here: 44.6 us
  Pallas kernels  43.1 us (96%)
  between operations  1.48 us (3%)
    pallas_call x1, Pallas kernels, per_device(): pl.pallas_call(functools.partial(mega_kernel, heads, n_rows, n_cols, logi...  39.7 us
    pallas_call x1, Pallas kernels, per_device(): pl.pallas_call(functools.partial(finish_kernel, heads, n_rows, logit_scal...  3.39 us

profile of v3, /device:TPU:1, one launch (start us, length us, event | category | flops | bytes accessed | tf_op | source)
XLA Modules:
  0.0 44.6 jit_solution(4780338873337888765)
XLA Ops:
  0.6 0.0 copy-start.5
  0.7 0.0 copy-start.2
  0.7 0.0 copy-start
  0.7 0.0 copy-start.1
  0.7 0.0 copy-start.4
  0.7 0.0 copy-start.3
  0.7 0.0 copy-start.6
  1.4 39.7 %mega.1 = (bf16[64,256,128]{2,1,0:T(8,128)(2,1)S(1)}, f32[7,8,128]{2,1,0:T(8,128)S(1)}, f32[6,8,128]{2,1,0:T(8,128)S(1)}, f32[16,128]{1,0:T(8,128)S(1)}) custom-call(s32[1]{0:T(128)S(6)} %copy.26.rc, bf16[64,256,128]{2,1,0:T(8,128)(2,1)} %pair_hbm.1, bf16[12,128]{1,0:T(8,128)(2,1)} %bitcast.21, f32[1,12]{1,0:T(1,128)} %bitcast.16, ...), custom_call_target="tpu_custom_call" | custom-call | tf_op jit(solution)/shard_map/mega/pallas_call | solution.py:668
  41.1 0.0 copy-done.5
  41.1 0.0 copy-done.2
  41.1 0.0 copy-done
  41.1 0.0 copy-done.1
  41.1 0.0 copy-done.4
  41.2 0.0 copy-done.3
  41.2 0.0 copy-done.6
  41.2 3.4 %finish.1 = (bf16[64,256,128]{2,1,0:T(8,128)(2,1)}, f32[8,192]{1,0:T(8,128)}, f32[3,8,48]{2,1,0:T(8,128)}, f32[3,4,8]{2,1,0:T(4,128)}, f32[8,192]{1,0:T(8,128)},...) custom-call(bf16[64,256,128]{2,1,0:T(8,128)(2,1)S(1)} %get-tuple-ele, ...), custom_call_target="tpu_custom_call" | custom-call | tf_op jit(solution)/shard_map/finish/pallas_call | solution.py:729
Async XLA Ops:
  0.6 40.5 %copy-start.5 = (f32[3,2048]{1,0:T(4,128)S(1)}, f32[3,2048]{1,0:T(4,128)}, u32[]{:S(2)}) copy-start(f32[3,2048]{1,0:T(4,128)} %shift_hbm.1) | copy-start | bytes 73732
  0.7 40.5 %copy-start.2 = (f32[3,3,2048]{2,1,0:T(4,128)S(1)}, f32[3,3,2048]{2,1,0:T(4,128)}, u32[]{:S(2)}) copy-start(f32[3,3,2048]{2,1,0:T(4,128)} %rot_hbm.1) | copy-start | bytes 221188
  0.7 40.5 %copy-start = (f32[3,96,256]{2,1,0:T(8,128)S(1)}, f32[3,96,256]{2,1,0:T(8,128)}, u32[]{:S(2)}) copy-start(f32[3,96,256]{2,1,0:T(8,128)} %vp_hbm.1) | copy-start | bytes 884740
  0.7 40.5 %copy-start.1 = (f32[3,48,256]{2,1,0:T(8,128)S(1)}, f32[3,48,256]{2,1,0:T(8,128)}, u32[]{:S(2)}) copy-start(f32[3,48,256]{2,1,0:T(8,128)} %kp_hbm.1) | copy-start | bytes 442372
  0.7 40.5 %copy-start.4 = (f32[3,48,64]{2,1,0:T(8,128)S(1)}, f32[3,48,64]{2,1,0:T(8,128)}, u32[]{:S(2)}) copy-start(f32[3,48,64]{2,1,0:T(8,128)} %qp_hbm.1) | copy-start | bytes 110596
  0.7 40.5 %copy-start.3 = (f32[3,96,64]{1,2,0:T(8,128)S(1)}, f32[3,96,64]{1,2,0:T(8,128)}, u32[]{:S(2)}) copy-start(f32[3,96,64]{1,2,0:T(8,128)} %param.28) | copy-start | bytes 221188
  0.7 40.5 %copy-start.6 = (f32[12]{0:T(128)S(1)}, f32[12]{0:T(128)}, u32[]{:S(2)}) copy-start(f32[12]{0:T(128)} %param.17) | copy-start | bytes 148

commit v4 on v3

--- a/solution.py
+++ b/solution.py
@@ -95,9 +95,9 @@
     bw, hw, gp_t, qt, kt, vt, qp, kp, vp, rot, shift, got, gpt = staged
     (
     pair, lbase, dbase, fb0, fb1, rd0, rd1, a_hi, a_lo, d_hi, d_lo,
-    wgf, wgb, qc, kc, wq, stat, stat_z, stat_m, stat_x,
+    wgf, wgb, qc, kc, wq, tt, qu, stat, stat_z, stat_m, stat_x,
     ks, ks_rx, sy, sy_rx, sz, sz_rx, qs, qs_rx, qz, qz_rx,
-    ar_c, ar_y, ar_x, ar_z, ar_s,
+    ar_y, ar_x, ar_z, ar_s,
     pair_sem, in_sem, s_send, s_recv, k_send, k_recv, y_send, y_recv, z_send, z_recv,
     q_send, q_recv, a_send, a_recv,
     ) = refs
@@ -113,6 +113,12 @@
     y_peer = lambda k: (row_of(zl, lax.rem(yy + k, YN), core), cl)
     z_peer = lambda k: (row_of(lax.rem(zl + k, ZL), yy, core), cl)
     x_peer = lambda k: (rw, lax.rem(xx + k, XN) * ZH + zh)
+    xc8 = xx * CORES + core
+
+    def plane_peer(k):
+        idx = lax.rem(xc8 + k, XN * CORES)
+        return (row_of(zl, yy, lax.rem(idx, CORES)), (idx // CORES) * ZH + zh)
+
     h_peer = (rw, xx * ZH + 1 - zh)
     z8 = zh * ZL + zl
 
@@ -123,7 +129,8 @@
     incoming = []
     for n, (source, target) in enumerate(zip(sources, staged)):
         incoming.append(pltpu.make_async_copy(source, target, in_sem.at[n]))
-        incoming[-1].start()
+    for n in (2, 0, 11, 3, 8, 7, 12, 9, 10, 4, 5, 6, 1):
+        incoming[n].start()
     parts = 4
     rows_per = n_rows // parts
     loads = []
@@ -133,9 +140,8 @@
         load.start()
         loads.append(load)
 
-    everyone = [sibling]
-    everyone += [y_peer(k) for k in range(1, YN)]
-    everyone += [x_peer(k) for k in range(1, XN)]
+    everyone = [y_peer(k) for k in range(1, YN)]
+    everyone += [plane_peer(k) for k in range(1, XN * CORES)]
     everyone += [ring_peer(k) for k in range(1, ZL * ZH)]
     barrier = pltpu.get_barrier_semaphore()
     for peer in everyone:
@@ -144,8 +150,8 @@
         )
 
     wgf[...] = jnp.zeros_like(wgf)
-    for copy in incoming:
-        copy.wait()
+    incoming[2].wait()
+    incoming[0].wait()
     w_all = bw[...].astype(F32)
     w_t = jnp.concatenate([w_all, jnp.zeros((PAD - heads, 128), F32)], 0)
     for h in range(heads):
@@ -155,6 +161,8 @@
         wgb[r, :PAD, :] = w_bf
         wgb[r, PAD:, :] = wgf[r * STRIDE + PAD : r * STRIDE + 2 * PAD, :].astype(BF16)
 
+    for n in (11, 3, 8, 7, 12, 9, 10, 4, 5, 6, 1):
+        incoming[n].wait()
     row_block = pl.multiple_of((rw // 2) * 128, 128)
     col_block = pl.multiple_of(cl * n_cols, 128)
 
@@ -296,6 +304,41 @@
     point_head, _ = group_mask(0, 8, 64)
     point_masks = [point_head == k for k in range(4)]
 
+    def query_group(pairs, masks, hi, lo, first):
+        blocks = lambda x: jnp.concatenate(
+            [jnp.where(m, x, jnp.zeros_like(x)) for m in masks], 1
+        )
+        lefts = lambda ref: jnp.concatenate(
+            [ref[pl.ds((first + k) * n_rows, n_rows)] for k in range(4)], 1
+        )
+        top = lefts(hi)
+        res = dot(jnp.concatenate([top, lefts(lo)], 0), blocks(pairs[0]), NT)
+        return res[:n_rows] + res[n_rows:] + dot(top, blocks(pairs[1]), NT)
+
+    both_rows = lambda r: jnp.concatenate(
+        [rd0[r * STRIDE : r * STRIDE + 2 * PAD, :], rd1[r * STRIDE : r * STRIDE + 2 * PAD, :]], 1
+    )
+    nearby = pltpu.roll(packed, 128 - 2 * PAD, 1) / pltpu.roll(packed, 128 - PAD, 1)
+    for h in range(heads):
+        e = lbase[h]
+        d = dbase[h] - nearby[:, h : h + 1]
+        dbase[h] = d
+        both = e * d
+        rows = pl.ds(h * n_rows, n_rows)
+        a_hi[rows], a_lo[rows] = split2(e)
+        d_hi[rows], d_lo[rows] = split2(both)
+        rd0[pl.ds(h, n_rows, stride=STRIDE), :] = both[:, :128]
+        rd1[pl.ds(h, n_rows, stride=STRIDE), :] = both[:, 128:]
+        rd0[pl.ds(PAD + h, n_rows, stride=STRIDE), :] = e[:, :128]
+        rd1[pl.ds(PAD + h, n_rows, stride=STRIDE), :] = e[:, 128:]
+    for g in range(3):
+        qu[g] = query_group(kb[g], query_masks, d_hi, d_lo, 4 * g)
+        qu[3 + g] = query_group(kb[g], query_masks, a_hi, a_lo, 4 * g)
+        qu[6 + g] = query_group(vb[g], point_masks, a_hi, a_lo, 4 * g)
+    for r in range(n_rows):
+        res = dot(jnp.concatenate(split2(both_rows(r)), 0), pair[r], NN)
+        tt[r] = res[: 2 * PAD] + res[2 * PAD :]
+
     def landed(dst, send, recv, peer):
         pltpu.make_async_remote_copy(
             src_ref=dst, dst_ref=dst, send_sem=send, recv_sem=recv,
@@ -318,9 +361,65 @@
     factor = jnp.concatenate([factor, pltpu.roll(factor, 64, 1)], 0)
     delta = jnp.concatenate([delta, pltpu.roll(delta, 64, 1)], 0)
 
+    def share(n, slots, place, count, peer, first):
+        for k in range(1, count):
+            sends.append(
+                push(
+                    ar_s.at[n], slots.at[place], a_send.at[first + k], a_recv.at[first + k],
+                    *peer(k)
+                )
+            )
+
+    def collect(slots, place, count, peer, first):
+        for k in range(1, count):
+            landed(
+                slots.at[lax.rem(place + count - k, count)], a_send.at[first + k],
+                a_recv.at[first + k], peer(k)
+            )
+        grand = slots[0]
+        for k in range(1, count):
+            grand = grand + slots[k]
+        return grand
+
+    moved = nearby - delta
+    row_factor = jnp.concatenate([factor, jnp.zeros_like(factor)], 0).T[:PAD]
+    row_moved = jnp.concatenate([moved[:, :PAD], jnp.zeros((n_rows, 128 - PAD), F32)], 1)
+    row_moved = jnp.concatenate([row_moved, jnp.zeros_like(row_moved)], 0).T[:PAD]
+    acc = jnp.zeros((PAD, 128), F32)
+    for r in range(n_rows):
+        term = tt[r, :PAD, :] + row_moved[:, r : r + 1] * tt[r, PAD:, :]
+        acc = acc + row_factor[:, r : r + 1] * term
+    lane_key = jnp.where(lane < 64, lane // PAD, (lane % PAD) // 4)
+    lane_point = (lane % 32) // 8
+
+    def spread(x, g, owner):
+        out = jnp.broadcast_to(x[:, 4 * g : 4 * g + 1], (n_rows, 128))
+        for k in range(1, 4):
+            out = jnp.where(owner == k, x[:, 4 * g + k : 4 * g + k + 1], out)
+        return out
+
+    distance, q_results = [], []
+    for g in range(3):
+        res = spread(factor, g, lane_key) * (qu[g] + spread(moved, g, lane_key) * qu[3 + g])
+        distance.append(jnp.sum(res * wq[g], axis=0, keepdims=True))
+        q_results.append(res)
+    acc = scale * acc
+    sub = lax.broadcasted_iota(jnp.int32, (PAD, 128), 0)
+    lane1 = lane_of((1, 128))
+    owner = jnp.where(lane1 < 112, (lane1 % PAD) // 4, (lane1 - 112) // 4)
+    dist_row = jnp.zeros((1, 128), F32)
+    for h in range(heads):
+        part = jnp.sum(jnp.where(owner == h % 4, distance[h // 4], 0.0), axis=1, keepdims=True)
+        dist_row = jnp.where(lane1 == h, part, dist_row)
+    acc = jnp.where(sub == heads, dist_row, acc)
+    ar_s[0] = acc
+    ar_z[z8] = acc
+
+    share(0, ar_z, z8, ZL * ZH, ring_peer, -1)
+
     def make_head(h):
         att = lbase[h] * factor[:, h : h + 1]
-        dl = att * (dbase[h] - delta[:, h : h + 1])
+        dl = att * (dbase[h] + moved[:, h : h + 1])
         rows = pl.ds(h * n_rows, n_rows)
         a_hi[rows], a_lo[rows] = split2(att)
         d_hi[rows], d_lo[rows] = split2(dl)
@@ -391,36 +490,18 @@
         make_head(h)
     key_group(1, qb[1], d_hi, d_lo, 4, 4)
     key_group(4, gb[1], a_hi, a_lo, 3, 3)
-    y_stage(0)
-    y_stage(3)
     for h in range(8, 12):
         make_head(h)
     key_group(2, qb[2], d_hi, d_lo, 8, 4)
     key_group(5, gb[2], a_hi, a_lo, 6, 3)
     key_group(6, gb[3], a_hi, a_lo, 9, 3)
-    y_stage(1)
-    y_stage(4)
-
-    def query_group(pairs, masks, hi, lo, first):
-        blocks = lambda x: jnp.concatenate(
-            [jnp.where(m, x, jnp.zeros_like(x)) for m in masks], 1
-        )
-        lefts = lambda ref: jnp.concatenate(
-            [ref[pl.ds((first + k) * n_rows, n_rows)] for k in range(4)], 1
-        )
-        top = lefts(hi)
-        res = dot(jnp.concatenate([top, lefts(lo)], 0), blocks(pairs[0]), NT)
-        return res[:n_rows] + res[n_rows:] + dot(top, blocks(pairs[1]), NT)
-
-    distance = []
+
+    for g in (0, 3, 1, 4, 2, 5, 6):
+        y_stage(g)
+    for g in range(3):
+        q_results.append(spread(factor, g, lane_point) * qu[6 + g])
     for g in range(6):
-        if g < 3:
-            res = query_group(kb[g], query_masks, d_hi, d_lo, 4 * g)
-        else:
-            res = query_group(vb[g - 3], point_masks, a_hi, a_lo, 4 * (g - 3))
-        if g < 3:
-            distance.append(jnp.sum(res * wq[g], axis=0, keepdims=True))
-        flat = res.reshape(XN, ZH, 8, 128)
+        flat = q_results[g].reshape(XN, ZH, 8, 128)
         for x in range(XN):
             for z in range(ZH):
                 qs[x, z, g] = flat[x, z]
@@ -431,93 +512,37 @@
                 q_send.at[k - 1], q_recv.at[k - 1], *x_peer(k)
             )
         )
-    y_stage(2)
-    y_stage(5)
-    y_stage(6)
-
-    both_rows = lambda r: jnp.concatenate(
-        [rd0[r * STRIDE : r * STRIDE + 2 * PAD, :], rd1[r * STRIDE : r * STRIDE + 2 * PAD, :]], 1
-    ).astype(BF16)
-    acc = jnp.zeros((PAD, 128), F32)
-    for r in range(n_rows):
-        acc = acc + dot(both_rows(r)[:PAD], pair[r], NN)
-    acc = scale * acc
-    sub = lax.broadcasted_iota(jnp.int32, (PAD, 128), 0)
-    lane1 = lane_of((1, 128))
-    owner = jnp.where(lane1 < 112, (lane1 % PAD) // 4, (lane1 - 112) // 4)
-    dist_row = jnp.zeros((1, 128), F32)
-    for h in range(heads):
-        part = jnp.sum(jnp.where(owner == h % 4, distance[h // 4], 0.0), axis=1, keepdims=True)
-        dist_row = jnp.where(lane1 == h, part, dist_row)
-    acc = jnp.where(sub == heads, dist_row, acc)
-    ar_s[0] = acc
-    sends.append(push(ar_s.at[0], ar_c, a_send.at[0], a_recv.at[0], *sibling))
-
     w_hi, w_lo = split2(scale * w_t)
 
     def pair_rows(first, count):
         for r in range(first, first + count):
-            a = both_rows(r)
+            a = both_rows(r).astype(BF16)
             lhs = jnp.concatenate([a, a[:PAD]], 0)
             rhs = jnp.concatenate([w_hi, wgb[r, PAD:, :], w_lo], 0)
             pg_out[r] = dot(lhs, rhs, TN).astype(BF16)
 
-    quarter = n_rows // 4
-    pair_rows(0, quarter)
-
-    landed(ar_c, a_send.at[0], a_recv.at[0], sibling)
-    ar_s[1] = ar_s[0] + ar_c[...]
-    ar_x[xx] = ar_s[1]
-    for k in range(1, XN):
-        sends.append(push(ar_s.at[1], ar_x.at[xx], a_send.at[k], a_recv.at[k], *x_peer(k)))
-
-    pair_rows(quarter, quarter)
+    pair_rows(0, n_rows)
     z_stage(0)
     z_stage(3)
     for k in range(1, XN):
         landed(qs_rx.at[k - 1], q_send.at[k - 1], q_recv.at[k - 1], x_peer(k))
     qz[...] = qs[xx] + qs_rx[0] + qs_rx[1] + qs_rx[2]
     sends.append(push(qz.at[1 - zh], qz_rx, q_send.at[3], q_recv.at[3], *h_peer))
-
-    pair_rows(2 * quarter, quarter)
-    z_stage(1)
-    for k in range(1, XN):
-        landed(ar_x.at[lax.rem(xx + XN - k, XN)], a_send.at[k], a_recv.at[k], x_peer(k))
-    ar_s[2] = ar_x[0] + ar_x[1] + ar_x[2] + ar_x[3]
-    ar_z[z8] = ar_s[2]
-    for k in range(1, ZL * ZH):
-        sends.append(
-            push(ar_s.at[2], ar_z.at[z8], a_send.at[6 + k], a_recv.at[6 + k], *ring_peer(k))
-        )
-
-    pair_rows(3 * quarter, quarter)
-    z_stage(4)
-    z_stage(2)
-    z_stage(5)
-    z_stage(6)
-    for k in range(1, ZL * ZH):
-        landed(
-            ar_z.at[lax.rem(z8 + ZL * ZH - k, ZL * ZH)], a_send.at[6 + k], a_recv.at[6 + k],
-            ring_peer(k),
-        )
-    grand = ar_z[0]
-    for k in range(1, ZL * ZH):
-        grand = grand + ar_z[k]
-    ar_s[3] = grand
-    ar_y[yy] = ar_s[3]
-    for k in range(1, YN):
-        sends.append(
-            push(ar_s.at[3], ar_y.at[yy], a_send.at[3 + k], a_recv.at[3 + k], *y_peer(k))
-        )
+    grand = collect(ar_z, z8, ZL * ZH, ring_peer, -1)
+    ar_s[1] = grand
+    ar_x[xc8] = grand
+    share(1, ar_x, xc8, XN * CORES, plane_peer, 6)
+    for g in (1, 4, 2, 5, 6):
+        z_stage(g)
+    grand = collect(ar_x, xc8, XN * CORES, plane_peer, 6)
+    ar_s[2] = grand
+    ar_y[yy] = grand
+    share(2, ar_y, yy, YN, y_peer, 13)
     landed(qz_rx, q_send.at[3], q_recv.at[3], h_peer)
     qf_out[...] = qz[zh] + qz_rx[...]
     for g in (0, 3, 1, 4, 2, 5, 6):
         last_stage(g)
-    for k in range(1, YN):
-        landed(
-            ar_y.at[lax.rem(yy + YN - k, YN)], a_send.at[3 + k], a_recv.at[3 + k], y_peer(k)
-        )
-    wr_out[...] = ar_y[0] + ar_y[1] + ar_y[2] + ar_y[3]
+    wr_out[...] = collect(ar_y, yy, YN, y_peer, 13)
     for copy in sends:
         copy.wait_send()
 
@@ -689,6 +714,8 @@
             pltpu.VMEM((heads, 32, n_rows), F32),
             pltpu.VMEM((heads, 32, n_cols), F32),
             pltpu.VMEM((3, n_rows, 128), F32),
+            pltpu.VMEM((n_rows, 2 * PAD, 128), F32),
+            pltpu.VMEM((9, n_rows, 128), F32),
             pltpu.VMEM((32, 128), F32),
             pltpu.VMEM((32, 128), F32),
             pltpu.VMEM((32, 128), F32),
@@ -703,18 +730,17 @@
             pltpu.VMEM((XN - 1, ZH, 6, 8, 128), F32),
             pltpu.VMEM((ZH, 6, 8, 128), F32),
             pltpu.VMEM((6, 8, 128), F32),
-            pltpu.VMEM((PAD, 128), F32),
             pltpu.VMEM((YN, PAD, 128), F32),
-            pltpu.VMEM((XN, PAD, 128), F32),
+            pltpu.VMEM((XN * CORES, PAD, 128), F32),
             pltpu.VMEM((ZL * ZH, PAD, 128), F32),
-            pltpu.VMEM((4, PAD, 128), F32),
+            pltpu.VMEM((3, PAD, 128), F32),
             dma((4,)), dma((13,)),
             dma((4,)), dma((4,)),
             dma((7,)), dma((7,)),
             dma((3, 7)), dma((3, 7)),
             dma((3, 7)), dma((3, 7)),
             dma((4,)), dma((4,)),
-            dma((14,)), dma((14,)),
+            dma((17,)), dma((17,)),
         ],
         compiler_params=pltpu.CompilerParams(
             collective_id=0, has_side_effects=True, vmem_limit_bytes=VMEM_LIMIT

time: 44.7 us -> 42.4 us (0.949)
  Pallas kernels: 43.1 us -> 40.8 us
    pallas_call x1, Pallas kernels: 39.7 us -> 37.4 us  [per_device(): pl.pallas_call(functools.partial(mega_kernel, heads, n_rows, n_cols, logi...]
where the time goes in v4:
time: 42.4 us; the launch traced here: 42.3 us
  Pallas kernels  40.8 us (96%)
  between operations  1.48 us (3%)
    pallas_call x1, Pallas kernels, per_device(): pl.pallas_call(functools.partial(mega_kernel, heads, n_rows, n_cols, logi...  37.4 us
    pallas_call x1, Pallas kernels, per_device(): pl.pallas_call(functools.partial(finish_kernel, heads, n_rows, logit_scal...  3.39 us

profile of v4, /device:TPU:1, one launch (start us, length us, event | category | flops | bytes accessed | tf_op | source)
XLA Modules:
  0.0 42.3 jit_solution(17495662767008825099)
XLA Ops:
  0.6 0.0 copy-start.5
  0.7 0.0 copy-start.2
  0.7 0.0 copy-start
  0.7 0.0 copy-start.1
  0.7 0.0 copy-start.4
  0.7 0.0 copy-start.3
  0.7 0.0 copy-start.6
  1.4 37.4 %mega.1 = (bf16[64,256,128]{2,1,0:T(8,128)(2,1)S(1)}, f32[7,8,128]{2,1,0:T(8,128)S(1)}, f32[6,8,128]{2,1,0:T(8,128)S(1)}, f32[16,128]{1,0:T(8,128)S(1)}) custom-call(s32[1]{0:T(128)S(6)} %copy.26.rc, bf16[64,256,128]{2,1,0:T(8,128)(2,1)} %pair_hbm.1, bf16[12,128]{1,0:T(8,128)(2,1)} %bitcast.21, f32[1,12]{1,0:T(1,128)} %bitcast.16, ...), custom_call_target="tpu_custom_call" | custom-call | tf_op jit(solution)/shard_map/mega/pallas_call | solution.py:693
  38.9 0.0 copy-done.5
  38.9 0.0 copy-done.2
  38.9 0.0 copy-done
  38.9 0.0 copy-done.1
  38.9 0.0 copy-done.4
  38.9 0.0 copy-done.3
  38.9 0.0 copy-done.6
  38.9 3.4 %finish.1 = (bf16[64,256,128]{2,1,0:T(8,128)(2,1)}, f32[8,192]{1,0:T(8,128)}, f32[3,8,48]{2,1,0:T(8,128)}, f32[3,4,8]{2,1,0:T(4,128)}, f32[8,192]{1,0:T(8,128)},...) custom-call(bf16[64,256,128]{2,1,0:T(8,128)(2,1)S(1)} %get-tuple-ele, ...), custom_call_target="tpu_custom_call" | custom-call | tf_op jit(solution)/shard_map/finish/pallas_call | solution.py:755
Async XLA Ops:
  0.6 38.2 %copy-start.5 = (f32[3,2048]{1,0:T(4,128)S(1)}, f32[3,2048]{1,0:T(4,128)}, u32[]{:S(2)}) copy-start(f32[3,2048]{1,0:T(4,128)} %shift_hbm.1) | copy-start | bytes 73732
  0.7 38.2 %copy-start.2 = (f32[3,3,2048]{2,1,0:T(4,128)S(1)}, f32[3,3,2048]{2,1,0:T(4,128)}, u32[]{:S(2)}) copy-start(f32[3,3,2048]{2,1,0:T(4,128)} %rot_hbm.1) | copy-start | bytes 221188
  0.7 38.2 %copy-start = (f32[3,96,256]{2,1,0:T(8,128)S(1)}, f32[3,96,256]{2,1,0:T(8,128)}, u32[]{:S(2)}) copy-start(f32[3,96,256]{2,1,0:T(8,128)} %vp_hbm.1) | copy-start | bytes 884740
  0.7 38.2 %copy-start.1 = (f32[3,48,256]{2,1,0:T(8,128)S(1)}, f32[3,48,256]{2,1,0:T(8,128)}, u32[]{:S(2)}) copy-start(f32[3,48,256]{2,1,0:T(8,128)} %kp_hbm.1) | copy-start | bytes 442372
  0.7 38.2 %copy-start.4 = (f32[3,48,64]{2,1,0:T(8,128)S(1)}, f32[3,48,64]{2,1,0:T(8,128)}, u32[]{:S(2)}) copy-start(f32[3,48,64]{2,1,0:T(8,128)} %qp_hbm.1) | copy-start | bytes 110596
  0.7 38.2 %copy-start.3 = (f32[3,96,64]{1,2,0:T(8,128)S(1)}, f32[3,96,64]{1,2,0:T(8,128)}, u32[]{:S(2)}) copy-start(f32[3,96,64]{1,2,0:T(8,128)} %param.28) | copy-start | bytes 221188
  0.7 38.2 %copy-start.6 = (f32[12]{0:T(128)S(1)}, f32[12]{0:T(128)}, u32[]{:S(2)}) copy-start(f32[12]{0:T(128)} %param.17) | copy-start | bytes 148

commit v5 on v4

--- a/solution.py
+++ b/solution.py
@@ -129,17 +129,19 @@
     incoming = []
     for n, (source, target) in enumerate(zip(sources, staged)):
         incoming.append(pltpu.make_async_copy(source, target, in_sem.at[n]))
-    for n in (2, 0, 11, 3, 8, 7, 12, 9, 10, 4, 5, 6, 1):
-        incoming[n].start()
     parts = 4
     rows_per = n_rows // parts
     loads = []
     for p in range(parts):
         piece = pl.ds(p * rows_per, rows_per)
-        load = pltpu.make_async_copy(pair_hbm.at[piece], pair.at[piece], pair_sem.at[p])
-        load.start()
-        loads.append(load)
-
+        loads.append(pltpu.make_async_copy(pair_hbm.at[piece], pair.at[piece], pair_sem.at[p]))
+    for n in (2, 0):
+        incoming[n].start()
+    loads[0].start()
+    for n in (11, 3, 8, 7, 12, 9, 10, 4, 5, 6, 1):
+        incoming[n].start()
+    for p in range(1, parts):
+        loads[p].start()
     everyone = [y_peer(k) for k in range(1, YN)]
     everyone += [plane_peer(k) for k in range(1, XN * CORES)]
     everyone += [ring_peer(k) for k in range(1, ZL * ZH)]
@@ -161,8 +163,26 @@
         wgb[r, :PAD, :] = w_bf
         wgb[r, PAD:, :] = wgf[r * STRIDE + PAD : r * STRIDE + 2 * PAD, :].astype(BF16)
 
+    def bias_rows(p):
+        loads[p].wait()
+        zero = jnp.zeros((2 * PAD, 128), BF16)
+        for i in range(0, rows_per, 2):
+            r = p * rows_per + i
+            left = jnp.concatenate(
+                [
+                    jnp.concatenate([wgb[r], zero], 1),
+                    jnp.concatenate([zero, wgb[r + 1]], 1),
+                ], 0
+            )
+            res = dot(left, jnp.concatenate([pair[r], pair[r + 1]], 1), NT)
+            for n in range(2):
+                rows = slice((r + n) * STRIDE, (r + n) * STRIDE + 2 * PAD)
+                fb0[rows, :] = res[2 * PAD * n : 2 * PAD * n + 2 * PAD, :128]
+                fb1[rows, :] = res[2 * PAD * n : 2 * PAD * n + 2 * PAD, 128:]
+
     for n in (11, 3, 8, 7, 12, 9, 10, 4, 5, 6, 1):
         incoming[n].wait()
+    bias_rows(0)
     row_block = pl.multiple_of((rw // 2) * 128, 128)
     col_block = pl.multiple_of(cl * n_cols, 128)
 
@@ -227,14 +247,8 @@
             jnp.concatenate([g0, g0, g1], 0), jnp.concatenate([v0, v1, v0], 0), TN
         )
 
-    for p in range(parts):
-        loads[p].wait()
-
-        for i in range(rows_per):
-            r = p * rows_per + i
-            res = dot(wgb[r], pair[r], NT)
-            fb0[r * STRIDE : r * STRIDE + 2 * PAD, :] = res[:, :128]
-            fb1[r * STRIDE : r * STRIDE + 2 * PAD, :] = res[:, 128:]
+    for p in range(1, parts):
+        bias_rows(p)
 
     limit = rc[0] - cl * n_cols
     valid = lane_of((n_rows, n_cols)) < limit
@@ -522,22 +536,25 @@
             pg_out[r] = dot(lhs, rhs, TN).astype(BF16)
 
     pair_rows(0, n_rows)
+    grand = collect(ar_z, z8, ZL * ZH, ring_peer, -1)
+    ar_s[1] = grand
+    ar_x[xc8] = grand
+    share(1, ar_x, xc8, XN * CORES, plane_peer, 6)
     z_stage(0)
     z_stage(3)
     for k in range(1, XN):
         landed(qs_rx.at[k - 1], q_send.at[k - 1], q_recv.at[k - 1], x_peer(k))
     qz[...] = qs[xx] + qs_rx[0] + qs_rx[1] + qs_rx[2]
     sends.append(push(qz.at[1 - zh], qz_rx, q_send.at[3], q_recv.at[3], *h_peer))
-    grand = collect(ar_z, z8, ZL * ZH, ring_peer, -1)
-    ar_s[1] = grand
-    ar_x[xc8] = grand
-    share(1, ar_x, xc8, XN * CORES, plane_peer, 6)
-    for g in (1, 4, 2, 5, 6):
-        z_stage(g)
+    z_stage(1)
+    z_stage(4)
+    z_stage(2)
+    z_stage(5)
     grand = collect(ar_x, xc8, XN * CORES, plane_peer, 6)
     ar_s[2] = grand
     ar_y[yy] = grand
     share(2, ar_y, yy, YN, y_peer, 13)
+    z_stage(6)
     landed(qz_rx, q_send.at[3], q_recv.at[3], h_peer)
     qf_out[...] = qz[zh] + qz_rx[...]
     for g in (0, 3, 1, 4, 2, 5, 6):
@@ -549,22 +566,18 @@
 
 def finish_kernel(
     heads, n_rows, scale, inner, coef_scale,
-    pg, kf, qf, wr, hw_hbm, qp_hbm, kp_hbm, vp_hbm, rot_hbm, shift_hbm, gpt_hbm,
+    pg, kf, qf, wr, hw, qp, kp, vp, rot, shift, gpt,
     pg_out, qgrad, qpgrad, qframe, kgrad, vgrad, kpgrad, vpgrad, kframe, weight, head_out,
-    hw, qp, kp, vp, rot, shift, gpt, turned, in_sem, sem,
+    turned, sem,
 ):
-    incoming = []
-    sources = (hw_hbm, qp_hbm, kp_hbm, vp_hbm, rot_hbm, shift_hbm, gpt_hbm)
-    for n, (source, target) in enumerate(zip(sources, (hw, qp, kp, vp, rot, shift, gpt))):
-        incoming.append(pltpu.make_async_copy(source, target, in_sem.at[n]))
-        incoming[-1].start()
-    copy = pltpu.make_async_copy(pg, pg_out, sem)
-    copy.start()
+    copies = []
+    for n in range(4):
+        piece = pl.ds(n * (n_rows // 4), n_rows // 4)
+        copies.append(pltpu.make_async_copy(pg.at[piece], pg_out.at[piece], sem.at[n]))
+        copies[-1].start()
     rw = lax.axis_index("row")
     cl = lax.axis_index("col")
     weight[...] = wr[:heads, :]
-    for load in incoming:
-        load.wait()
     sig = 1.0 / (1.0 + jnp.exp(-hw[...]))
     head_out[...] = wr[heads : heads + 1, :heads] * (-coef_scale) * sig
     coef = coef_scale * soft(hw[...])
@@ -660,7 +673,8 @@
             entries.append(add_all(dkg[x] * points[y]) + add_all(dvg[x] * vpoints[y]))
         entries.append(add_all(dkg[x]) + add_all(dvg[x]))
     frame_out(kframe, entries)
-    copy.wait()
+    for copy in copies:
+        copy.wait()
 
 
 def per_device(
@@ -756,7 +770,7 @@
         functools.partial(
             finish_kernel, heads, n_rows, logit_scale, inner_scale, coef_scale
         ),
-        in_specs=[vm] * 4 + [hbm] * 7,
+        in_specs=[vm] * 11,
         out_specs=[hbm] + [vm] * 10,
         out_shape=[
             jax.ShapeDtypeStruct(pair_rep.shape, BF16),
@@ -771,7 +785,7 @@
             f32(heads, channels),
             f32(1, heads),
         ],
-        scratch_shapes=[*[like(x) for x in late], pltpu.VMEM((128, 128), F32), dma((7,)), dma],
+        scratch_shapes=[pltpu.VMEM((128, 128), F32), dma((4,))],
         compiler_params=pltpu.CompilerParams(vmem_limit_bytes=VMEM_LIMIT),
         name="finish",
     )(pg, kf, qf, wr, *late)

time: 42.4 us -> 39.9 us (0.941)
  Pallas kernels: 40.8 us -> 38.3 us
    pallas_call x1, Pallas kernels: 37.4 us -> 35 us  [per_device(): pl.pallas_call(functools.partial(mega_kernel, heads, n_rows, n_cols, logi...]
where the time goes in v5:
time: 39.9 us; the launch traced here: 39.8 us
  Pallas kernels  38.3 us (96%)
  between operations  1.48 us (4%)
    pallas_call x1, Pallas kernels, per_device(): pl.pallas_call(functools.partial(mega_kernel, heads, n_rows, n_cols, logi...  35 us
    pallas_call x1, Pallas kernels, per_device(): pl.pallas_call(functools.partial(finish_kernel, heads, n_rows, logit_scal...  3.32 us

profile of v5, /device:TPU:1, one launch (start us, length us, event | category | flops | bytes accessed | tf_op | source)
XLA Modules:
  0.0 39.8 jit_solution(14657103851680252353)
XLA Ops:
  0.6 0.0 copy-start.5
  0.7 0.0 copy-start.2
  0.7 0.0 copy-start
  0.7 0.0 copy-start.1
  0.7 0.0 copy-start.4
  0.7 0.0 copy-start.3
  0.7 0.0 copy-start.6
  1.4 35.0 %mega.1 = (bf16[64,256,128]{2,1,0:T(8,128)(2,1)S(1)}, f32[7,8,128]{2,1,0:T(8,128)S(1)}, f32[6,8,128]{2,1,0:T(8,128)S(1)}, f32[16,128]{1,0:T(8,128)S(1)}) custom-call(s32[1]{0:T(128)S(6)} %copy.26.rc, bf16[64,256,128]{2,1,0:T(8,128)(2,1)} %pair_hbm.1, bf16[12,128]{1,0:T(8,128)(2,1)} %bitcast.21, f32[1,12]{1,0:T(1,128)} %bitcast.16, ...), custom_call_target="tpu_custom_call" | custom-call | tf_op jit(solution)/shard_map/mega/pallas_call | solution.py:707
  36.4 0.0 copy-done.5
  36.4 0.0 copy-done.2
  36.5 0.0 copy-done
  36.5 0.0 copy-done.1
  36.5 0.0 copy-done.4
  36.5 0.0 copy-done.3
  36.5 0.0 copy-done.6
  36.5 3.3 %finish.1 = (bf16[64,256,128]{2,1,0:T(8,128)(2,1)}, f32[8,192]{1,0:T(8,128)}, f32[3,8,48]{2,1,0:T(8,128)}, f32[3,4,8]{2,1,0:T(4,128)}, f32[8,192]{1,0:T(8,128)},...) custom-call(bf16[64,256,128]{2,1,0:T(8,128)(2,1)S(1)} %get-tuple-ele, ...), custom_call_target="tpu_custom_call" | custom-call | tf_op jit(solution)/shard_map/finish/pallas_call | solution.py:769
Async XLA Ops:
  0.6 35.8 %copy-start.5 = (f32[3,2048]{1,0:T(4,128)S(1)}, f32[3,2048]{1,0:T(4,128)}, u32[]{:S(2)}) copy-start(f32[3,2048]{1,0:T(4,128)} %shift.1) | copy-start | bytes 73732
  0.7 35.8 %copy-start.2 = (f32[3,3,2048]{2,1,0:T(4,128)S(1)}, f32[3,3,2048]{2,1,0:T(4,128)}, u32[]{:S(2)}) copy-start(f32[3,3,2048]{2,1,0:T(4,128)} %rot.1) | copy-start | bytes 221188
  0.7 35.8 %copy-start = (f32[3,96,256]{2,1,0:T(8,128)S(1)}, f32[3,96,256]{2,1,0:T(8,128)}, u32[]{:S(2)}) copy-start(f32[3,96,256]{2,1,0:T(8,128)} %vp.1) | copy-start | bytes 884740
  0.7 35.8 %copy-start.1 = (f32[3,48,256]{2,1,0:T(8,128)S(1)}, f32[3,48,256]{2,1,0:T(8,128)}, u32[]{:S(2)}) copy-start(f32[3,48,256]{2,1,0:T(8,128)} %kp.1) | copy-start | bytes 442372
  0.7 35.8 %copy-start.4 = (f32[3,48,64]{2,1,0:T(8,128)S(1)}, f32[3,48,64]{2,1,0:T(8,128)}, u32[]{:S(2)}) copy-start(f32[3,48,64]{2,1,0:T(8,128)} %qp.1) | copy-start | bytes 110596
  0.7 35.8 %copy-start.3 = (f32[3,96,64]{1,2,0:T(8,128)S(1)}, f32[3,96,64]{1,2,0:T(8,128)}, u32[]{:S(2)}) copy-start(f32[3,96,64]{1,2,0:T(8,128)} %param.28) | copy-start | bytes 221188
  0.7 35.8 %copy-start.6 = (f32[12]{0:T(128)S(1)}, f32[12]{0:T(128)}, u32[]{:S(2)}) copy-start(f32[12]{0:T(128)} %param.17) | copy-start | bytes 148

commit v6 on v5

--- a/solution.py
+++ b/solution.py
@@ -87,12 +87,12 @@
 
 def mega_kernel(
     heads, n_rows, n_cols, scale, inner, coef_scale,
-    rc, pair_hbm, *refs,
+    pair_hbm, *refs,
 ):
-    sources, refs = refs[:13], refs[13:]
+    sources, refs = refs[:14], refs[14:]
     pg_out, kf_out, qf_out, wr_out = refs[:4]
-    staged, refs = refs[4:17], refs[17:]
-    bw, hw, gp_t, qt, kt, vt, qp, kp, vp, rot, shift, got, gpt = staged
+    staged, refs = refs[4:18], refs[18:]
+    bw, hw, gp_t, qt, kt, vt, qp, kp, vp, rot, shift, got, gpt, rc = staged
     (
     pair, lbase, dbase, fb0, fb1, rd0, rd1, a_hi, a_lo, d_hi, d_lo,
     wgf, wgb, qc, kc, wq, tt, qu, stat, stat_z, stat_m, stat_x,
@@ -138,7 +138,7 @@
     for n in (2, 0):
         incoming[n].start()
     loads[0].start()
-    for n in (11, 3, 8, 7, 12, 9, 10, 4, 5, 6, 1):
+    for n in (11, 3, 8, 7, 12, 9, 10, 4, 5, 6, 1, 13):
         incoming[n].start()
     for p in range(1, parts):
         loads[p].start()
@@ -180,7 +180,7 @@
                 fb0[rows, :] = res[2 * PAD * n : 2 * PAD * n + 2 * PAD, :128]
                 fb1[rows, :] = res[2 * PAD * n : 2 * PAD * n + 2 * PAD, 128:]
 
-    for n in (11, 3, 8, 7, 12, 9, 10, 4, 5, 6, 1):
+    for n in (11, 3, 8, 7, 12, 9, 10, 4, 5, 6, 1, 13):
         incoming[n].wait()
     bias_rows(0)
     row_block = pl.multiple_of((rw // 2) * 128, 128)
@@ -250,7 +250,7 @@
     for p in range(1, parts):
         bias_rows(p)
 
-    limit = rc[0] - cl * n_cols
+    limit = rc[...] - cl * n_cols
     valid = lane_of((n_rows, n_cols)) < limit
     lane = lane_of((n_rows, 128))
     packed = jnp.ones((n_rows, 128), F32)
@@ -701,14 +701,17 @@
     inputs = (
         bias_weight.T, hw, grad_pair.transpose(1, 0, 2), queries.T, key_vectors, values,
         query_points, key_points, value_points, rotations, translations, grad_output.T, gpt,
+        residue_count.reshape(1, 1),
     )
     like = lambda x: pltpu.VMEM(x.shape, x.dtype)
-    inputs = tuple(pltpu.with_memory_space_constraint(x, pltpu.HBM) for x in inputs)
+    inputs = tuple(
+        pltpu.with_memory_space_constraint(x, pltpu.HBM) for x in inputs[:-1]
+    ) + inputs[-1:]
     pg, kf, qf, wr = pl.pallas_call(
         functools.partial(
             mega_kernel, heads, n_rows, n_cols, logit_scale, inner_scale, coef_scale
         ),
-        in_specs=[pl.BlockSpec(memory_space=pltpu.SMEM), *[hbm] * 14],
+        in_specs=[hbm] * 14 + [pl.BlockSpec(memory_space=pl.ANY)],
         out_specs=[vm] * 4,
         out_shape=[
             pltpu.VMEM(pair_rep.shape, BF16),
@@ -748,7 +751,7 @@
             pltpu.VMEM((XN * CORES, PAD, 128), F32),
             pltpu.VMEM((ZL * ZH, PAD, 128), F32),
             pltpu.VMEM((3, PAD, 128), F32),
-            dma((4,)), dma((13,)),
+            dma((4,)), dma((14,)),
             dma((4,)), dma((4,)),
             dma((7,)), dma((7,)),
             dma((3, 7)), dma((3, 7)),
@@ -761,7 +764,7 @@
         ),
         name="mega",
     )(
-        residue_count, pair_rep, *inputs
+        pair_rep, *inputs
     )
     share = 8
     late = (hw, query_points, key_points, value_points, rotations, translations, gpt)

time: 39.9 us -> 39.5 us (0.990)
  Pallas kernels: 38.3 us -> 37.9 us
    pallas_call x1, Pallas kernels: 35 us -> 34.6 us  [per_device(): pl.pallas_call(functools.partial(mega_kernel, heads, n_rows, n_cols, logi...]
where the time goes in v6:
time: 39.5 us; the launch traced here: 39.4 us
  Pallas kernels  37.9 us (96%)
  between operations  1.48 us (4%)
    pallas_call x1, Pallas kernels, per_device(): pl.pallas_call(functools.partial(mega_kernel, heads, n_rows, n_cols, logi...  34.6 us
    pallas_call x1, Pallas kernels, per_device(): pl.pallas_call(functools.partial(finish_kernel, heads, n_rows, logit_scal...  3.32 us

profile of v6, /device:TPU:1, one launch (start us, length us, event | category | flops | bytes accessed | tf_op | source)
XLA Modules:
  0.0 39.4 jit_solution(14210744428747702097)
XLA Ops:
  0.6 0.0 copy-start.5
  0.7 0.0 copy-start.2
  0.7 0.0 copy-start
  0.7 0.0 copy-start.1
  0.7 0.0 copy-start.4
  0.7 0.0 copy-start.3
  0.7 0.0 copy-start.6
  1.4 34.6 %mega.1 = (bf16[64,256,128]{2,1,0:T(8,128)(2,1)S(1)}, f32[7,8,128]{2,1,0:T(8,128)S(1)}, f32[6,8,128]{2,1,0:T(8,128)S(1)}, f32[16,128]{1,0:T(8,128)S(1)}) custom-call(bf16[64,256,128]{2,1,0:T(8,128)(2,1)} %pair_hbm.1, bf16[12,128]{1,0:T(8,128)(2,1)} %bitcast.23, f32[1,12]{1,0:T(1,128)} %bitcast.18, bf16[12,64,128]{2,1,0:T(8,128)(2,1)} %bitcast.20, ...), custom_call_target="tpu_custom_call" | custom-call | tf_op jit(solution)/shard_map/mega/pallas_call | solution.py:710
  36.0 0.0 copy-done.5
  36.0 0.0 copy-done.2
  36.0 0.0 copy-done
  36.0 0.0 copy-done.1
  36.0 0.0 copy-done.4
  36.0 0.0 copy-done.3
  36.1 0.0 copy-done.6
  36.1 3.3 %finish.1 = (bf16[64,256,128]{2,1,0:T(8,128)(2,1)}, f32[8,192]{1,0:T(8,128)}, f32[3,8,48]{2,1,0:T(8,128)}, f32[3,4,8]{2,1,0:T(4,128)}, f32[8,192]{1,0:T(8,128)},...) custom-call(bf16[64,256,128]{2,1,0:T(8,128)(2,1)S(1)} %get-tuple-ele, ...), custom_call_target="tpu_custom_call" | custom-call | tf_op jit(solution)/shard_map/finish/pallas_call | solution.py:772
Async XLA Ops:
  0.6 35.3 %copy-start.5 = (f32[3,2048]{1,0:T(4,128)S(1)}, f32[3,2048]{1,0:T(4,128)}, u32[]{:S(2)}) copy-start(f32[3,2048]{1,0:T(4,128)} %shift.1) | copy-start | bytes 73732
  0.7 35.3 %copy-start.2 = (f32[3,3,2048]{2,1,0:T(4,128)S(1)}, f32[3,3,2048]{2,1,0:T(4,128)}, u32[]{:S(2)}) copy-start(f32[3,3,2048]{2,1,0:T(4,128)} %rot.1) | copy-start | bytes 221188
  0.7 35.3 %copy-start = (f32[3,96,256]{2,1,0:T(8,128)S(1)}, f32[3,96,256]{2,1,0:T(8,128)}, u32[]{:S(2)}) copy-start(f32[3,96,256]{2,1,0:T(8,128)} %vp.1) | copy-start | bytes 884740
  0.7 35.3 %copy-start.1 = (f32[3,48,256]{2,1,0:T(8,128)S(1)}, f32[3,48,256]{2,1,0:T(8,128)}, u32[]{:S(2)}) copy-start(f32[3,48,256]{2,1,0:T(8,128)} %kp.1) | copy-start | bytes 442372
  0.7 35.3 %copy-start.4 = (f32[3,48,64]{2,1,0:T(8,128)S(1)}, f32[3,48,64]{2,1,0:T(8,128)}, u32[]{:S(2)}) copy-start(f32[3,48,64]{2,1,0:T(8,128)} %qp.1) | copy-start | bytes 110596
  0.7 35.3 %copy-start.3 = (f32[3,96,64]{1,2,0:T(8,128)S(1)}, f32[3,96,64]{1,2,0:T(8,128)}, u32[]{:S(2)}) copy-start(f32[3,96,64]{1,2,0:T(8,128)} %param.28) | copy-start | bytes 221188
  0.7 35.3 %copy-start.6 = (f32[12]{0:T(128)S(1)}, f32[12]{0:T(128)}, u32[]{:S(2)}) copy-start(f32[12]{0:T(128)} %param.17) | copy-start | bytes 148
